TPU v7x, 16 devices: a whole 2x2x2 slice. The times are simulated.
16 devices in a mesh: f: 2 (over z), h: 8 (over y, x, core).
Axes of the slice: x: 2, y: 2, z: 2, core: 2. Of those that a mesh axis runs over, the one named last changes fastest.
Arguments:
- x: bfloat16 [4096, 3072], P(None, 'h')
- g1: float32 [3072], P('h')
- g2: float32 [3072], P('h')
- w_gate: bfloat16 [3072, 8192], P('h', 'f')
- w_up: bfloat16 [3072, 8192], P('h', 'f')
- w_down: bfloat16 [8192, 3072], P('f', 'h')
- o: bfloat16 [4096, 3072], P(None, 'f')
- w_o: bfloat16 [3072, 3072], P('f', 'h')
- w_qkv: bfloat16 [3072, 5120], P('h', 'f')
Outputs:
- output 1: bfloat16 [4096, 3072], P(None, 'h')
- output 2: bfloat16 [4096, 5120], P(None, 'f')
All inputs are finite; a program needn't handle non-finite values.
Results may differ from a plain program's by a relative error of at most 0.0039825.
Values are sent between devices in bfloat16 or wider.
A program may use at most 1 GiB of HBM per device.

v0:
```python
import jax
import jax.numpy as jnp
from jax import lax
from jax.sharding import PartitionSpec as P

EPS = 1e-6


def _dot(a, b):
    return jnp.dot(a, b, preferred_element_type=jnp.float32)


def _norm(x, g, d):
    xf = x.astype(jnp.float32)
    ss = lax.psum(jnp.sum(xf * xf, axis=-1, keepdims=True), 'h')
    r = lax.rsqrt(ss / d + EPS)
    return (xf * r * g).astype(jnp.bfloat16)


def solution(mesh):
    h = mesh.shape['h']

    def body(x, g1, g2, w_gate, w_up, w_down, o, w_o, w_qkv):
        d = x.shape[1] * h
        n = _norm(x, g1, d)
        gt, up = lax.psum((_dot(n, w_gate), _dot(n, w_up)), 'h')
        a = (jax.nn.silu(gt) * up).astype(jnp.bfloat16)
        y = lax.psum(_dot(a, w_down) + _dot(o, w_o), 'f')
        x_next = (x.astype(jnp.float32) + y).astype(jnp.bfloat16)
        n1 = _norm(x_next, g2, d)
        qkv = lax.psum(_dot(n1, w_qkv), 'h').astype(jnp.bfloat16)
        return x_next, qkv

    in_specs = (P(None, 'h'), P('h'), P('h'), P('h', 'f'), P('h', 'f'), P('f', 'h'),
                P(None, 'f'), P('f', 'h'), P('h', 'f'))
    return jax.shard_map(body, mesh=mesh, in_specs=in_specs,
                         out_specs=(P(None, 'h'), P(None, 'f')), check_vma=False)
```

profile of v0, /device:TPU:0, one launch (start us, length us, event | category | flops | bytes accessed | tf_op | source)
XLA Modules:
  0.0 2633.2 jit_solution(6214880211332337621)
XLA Ops:
  7.2 0.0 copy-start
  7.2 0.0 all-reduce.5.cloned.1.call-start
  7.2 2.7 fusion.5
  10.0 25.8 psum.42
  35.8 0.0 copy-done
  35.8 27.5 %fusion.15 = f32[4096,4096]{1,0:T(8,128)} fusion(bf16[384,4096]{1,0:T(8,128)(2,1)S(1)} %copy-done, bf16[4096,384]{1,0:T(8,128)(2,1)} %param.9, f32[384]{0:T(512)} %param.10, f32[4096]{0:T(1024)S(1)} %bitcast.12), kind=kOutput, calls=%fused_computation.19 | convolution fusion | flops 12891193344 | bytes 73418240 | tf_op jit(solution)/shard_map/dot_general | solution.py:10
  63.3 0.0 copy-start.2
  63.3 0.0 copy-start.3
  63.3 0.0 all-reduce.5.cloned.1.call-update
  63.3 0.0 all-reduce.7.cloned.1.call-start
  63.4 1.8 copy-done.2
  65.2 0.0 copy-done.3
  65.2 27.5 %fusion.13 = f32[4096,4096]{1,0:T(8,128)} fusion(bf16[384,4096]{1,0:T(8,128)(2,1)} %param.13, bf16[4096,384]{1,0:T(8,128)(2,1)S(1)} %copy-done.2, f32[384]{0:T(512)S(1)} %copy-done.3, f32[4096]{0:T(1024)S(1)} %bitcast.13), kind=kOutput, calls=%fused_computation.18 | convolution fusion | flops 12891193344 | bytes 73418240 | tf_op jit(solution)/shard_map/dot_general | solution.py:10
  92.7 0.0 all-reduce.7.cloned.1.call-update
  92.7 0.2 all-reduce.9.cloned.1.call-start
  93.0 11.6 fusion.19
  104.6 708.4 %all-reduce.5.cloned.1.call-done = f32[4096,4096]{1,0:T(8,128)} async-done(((f32[4096,4096]{1,0:T(8,128)}), f32[4096,4096]{1,0:T(8,128)}) %all-reduce.5.cloned.1.call-update) | async-done | bytes 67108880 | tf_op jit(solution)/shard_map/psum | solution.py:26
  813.0 754.1 %all-reduce.7.cloned.1.call-done = f32[4096,4096]{1,0:T(8,128)} async-done(((f32[4096,4096]{1,0:T(8,128)}), f32[4096,4096]{1,0:T(8,128)}) %all-reduce.7.cloned.1.call-update) | async-done | bytes 67108880 | tf_op jit(solution)/shard_map/psum | solution.py:26
  1567.1 47.9 %fusion.1 = f32[4096,384]{1,0:T(8,128)} fusion(f32[4096,384]{1,0:T(8,128)} %fusion.19, bf16[4096,384]{1,0:T(8,128)(2,1)} %param.14, f32[4096,4096]{1,0:T(8,128)} %all-reduce.7.cloned.1.call-done, f32[4096,4096]{1,0:T(8,128)} %all-reduce.5.cloned.1.call-done), kind=kOutput, calls=%fused_computation.7 | convolution fusion | flops 12987138048 | bytes 149946368 | tf_op jit(solution)/shard_map/dot_general | solution.py:10
  1615.1 0.0 all-reduce.9.cloned.1.call-update
  1615.1 0.0 copy-start.4
  1615.1 149.3 %all-reduce.9.cloned.1.call-done = f32[4096,384]{1,0:T(8,128)} async-done(((f32[4096,384]{1,0:T(8,128)}), f32[4096,384]{1,0:T(8,128)}) %all-reduce.9.cloned.1.call-update) | async-done | bytes 6291472 | tf_op jit(solution)/shard_map/psum | solution.py:28
  1764.4 5.4 fusion.2
  1769.8 23.7 psum.46
  1793.6 0.0 copy-done.4
  1793.6 20.9 fusion.9
  1814.5 0.0 copy-start.1
  1814.5 812.1 %all-reduce.10 = bf16[4096,2560]{1,0:T(8,128)(2,1)} all-reduce(f32[4096,2560]{1,0:T(8,128)} %fusion.9), channel_id=1, replica_groups=mesh['f'=2,'h'=8] {'h'}, use_global_device_ids=true, to_apply=%region_7.8 | all-reduce | flops 10485760 | bytes 62914560 | tf_op jit(solution)/shard_map/psum | solution.py:31
  2626.6 0.0 copy-done.1
  (2 shorter events, 0.1 us)
Async XLA Ops:
  7.2 28.6 %copy-start = (bf16[384,4096]{1,0:T(8,128)(2,1)S(1)}, bf16[384,4096]{1,0:T(8,128)(2,1)}, u32[]{:S(2)}) copy-start(bf16[384,4096]{1,0:T(8,128)(2,1)} %param.12) | copy-start | bytes 9437188
  7.2 805.8 %all-reduce.5.cloned.1.call-start = ((), (), s32[]{:S(2)}) async-start(), calls=%async_computation | async-start | bytes 134217728 | tf_op jit(solution)/shard_map/psum | solution.py:26
  63.3 1.9 copy-start.2
  63.3 1.9 copy-start.3
  63.3 1503.8 %all-reduce.7.cloned.1.call-start = ((), (), s32[]{:S(2)}) async-start(), calls=%async_computation.1 | async-start | bytes 134217728 | tf_op jit(solution)/shard_map/psum | solution.py:26
  92.7 1671.7 %all-reduce.9.cloned.1.call-start = ((), (), s32[]{:S(2)}) async-start(), calls=%async_computation.2 | async-start | bytes 12582912 | tf_op jit(solution)/shard_map/psum | solution.py:28
  1615.1 178.5 %copy-start.4 = (f32[384]{0:T(512)S(1)}, f32[384]{0:T(512)}, u32[]{:S(2)}) copy-start(f32[384]{0:T(512)} %param.11) | copy-start | bytes 4612
  1814.5 812.1 %copy-start.1 = (bf16[384,4096]{1,0:T(8,128)(2,1)S(1)}, bf16[384,4096]{1,0:T(8,128)(2,1)}, u32[]{:S(2)}) copy-start(bf16[384,4096]{1,0:T(8,128)(2,1)} %param.12) | copy-start | bytes 9437188
Sparse Core Ops, SparseCore 0:
  63.4 749.5 all-reduce.4
  816.8 750.3 all-reduce.6
  1615.2 149.1 all-reduce.8
where the time goes:
time: 2630 us
  waiting for transfers between devices  1610 us (61%)
  blocking collectives  862 us (33%)
  matrix products  136 us (5%)
    psum x2, waiting for transfers between devices, body(): gt, up = lax.psum((_dot(n, w_gate), _dot(n, w_up)), 'h')  1460 us
    psum x1, blocking collectives, body(): qkv = lax.psum(_dot(n1, w_qkv), 'h').astype(jnp.bfloat16)  812 us
    psum x1, waiting for transfers between devices, body(): y = lax.psum(_dot(a, w_down) + _dot(o, w_o), 'f')  149 us
    dot_general x5, matrix products, _dot(): return jnp.dot(a, b, preferred_element_type=jnp.float32)  136 us
  transfers between devices with their start and end apart: 3, of which 3 were waited for; matrix products, arithmetic and copies ran while one was open for 1% of the time, Pallas kernels for 0%

commit v1 on v0

v1 whole, which is shorter than its diff:
```python
import jax
import jax.numpy as jnp
from jax import lax
from jax.experimental import pallas as pl
from jax.experimental.pallas import tpu as pltpu
from jax.sharding import PartitionSpec as P

EPS = 1e-6
BF, F32 = jnp.bfloat16, jnp.float32
MESH = pl.DeviceIdType.MESH
NREMOTE, NLOCAL = 176, 96

T, D, FF, HD, Q = 4096, 3072, 8192, 3072, 5120
B = D // 8
R = T // 4
Z = R // 2
FP = FF // 2
PIECES = 4
PC = FP // 2 // PIECES
K2 = FP + HD // 2
S = 128
QC = Q // 4
CH = 256


def _dot(a, b):
    return jnp.dot(a, b, preferred_element_type=F32)


def _kernel(x, g, wg, wu, wd, o, wo, wq, xo, qo, dl, ql,
            A, N, W, act, ys, yr, yo, gv, send, recv, loc):
    h = lax.axis_index('h')
    z = lax.axis_index('f')
    iy, ix, ic = lax.div(h, 4), lax.rem(lax.div(h, 2), 2), lax.rem(h, 2)

    def dev(kx, ky, kc):
        py = 1 - iy if ky else iy
        px = 1 - ix if kx else ix
        pc = 1 - ic if kc else ic
        return {'h': py * 4 + px * 2 + pc}

    XN, YN, CN, YCN, ZN = dev(1, 0, 0), dev(0, 1, 0), dev(0, 0, 1), dev(0, 1, 1), {'f': 1 - z}
    count = [0, 0]
    sends = []

    def put(src, dst, to):
        i = count[0]
        count[0] += 1
        c = pltpu.make_async_remote_copy(src, dst, send.at[i], recv.at[i], device_id=to, device_id_type=MESH)
        c.start()
        sends.append(c)
        return c

    def load(src, dst):
        i = count[1]
        count[1] += 1
        c = pltpu.make_async_copy(src, dst, loc.at[i])
        c.start()
        return c

    def settle(cs):
        for c in cs:
            c.wait_send()
            sends[:] = [d for d in sends if d is not c]

    def al(v, m):
        return pl.multiple_of(v, m)

    def ds(start, size, m):
        return pl.ds(al(start, m), size)

    def quarter(py, pc):
        return pc * (2 * R) + py * R

    mine = quarter(iy, ic)
    zr = ds(z * Z, Z, Z)
    zo = ds((1 - z) * Z, Z, Z)

    bar = pltpu.get_barrier_semaphore()
    for k in range(1, 8):
        pl.semaphore_signal(bar, inc=1, device_id=dev(k & 1, (k >> 1) & 1, k >> 2), device_id_type=MESH)
    pl.semaphore_signal(bar, inc=1, device_id=ZN, device_id_type=MESH)
    pl.semaphore_wait(bar, 8)

    def col(p):
        return pl.ds(p * B, B)

    x4 = put(x.at[ds(quarter(iy, 1 - ic), R, R), :], A.at[:, col(4)], CN)
    x2 = put(x.at[ds(quarter(1 - iy, ic) + z * Z, Z, Z), :], A.at[zr, col(2)], YN)
    x6 = put(x.at[ds(quarter(1 - iy, 1 - ic) + z * Z, Z, Z), :], A.at[zr, col(6)], YCN)
    x1 = put(x.at[ds(mine + z * Z, Z, Z), :], A.at[zr, col(1)], XN)
    x0 = load(x.at[ds(mine, R, R), :], A.at[:, col(0)])

    def wrow(j, a, n):
        return pl.ds(j * D + a, n)

    wl, wx, wyo, wyf, wc = {}, {}, {}, {}, {}

    def w_load(j):
        c0 = ds(ix * (FP // 2) + j * PC, PC, PC)
        wl[j] = [load(wg.at[:, c0], W.at[wrow(j, 0, B), pl.ds(0, PC)]),
                 load(wu.at[:, c0], W.at[wrow(j, 0, B), pl.ds(PC, PC)])]

    def w_x(j):
        c1 = ds((1 - ix) * (FP // 2) + j * PC, PC, PC)
        wx[j] = [put(wg.at[:, c1], W.at[wrow(j, B, B), pl.ds(0, PC)], XN),
                 put(wu.at[:, c1], W.at[wrow(j, B, B), pl.ds(PC, PC)], XN)]

    def w_yown(j):
        for c in wl[j]:
            c.wait()
        wyo[j] = put(W.at[wrow(j, 0, B), :], W.at[wrow(j, 2 * B, B), :], YN)

    def w_xgot(j):
        for c in wx[j]:
            c.wait_recv()
        wyf[j] = put(W.at[wrow(j, B, B), :], W.at[wrow(j, 3 * B, B), :], YN)
        wc[j] = [put(W.at[wrow(j, 0, 2 * B), :], W.at[wrow(j, 4 * B, 2 * B), :], CN)]

    def w_ygot(j):
        wyo[j].wait_recv()
        wc[j].append(put(W.at[wrow(j, 2 * B, B), :], W.at[wrow(j, 6 * B, B), :], CN))
        wyf[j].wait_recv()
        wc[j].append(put(W.at[wrow(j, 3 * B, B), :], W.at[wrow(j, 7 * B, B), :], CN))

    for j in range(PIECES):
        w_load(j)
    w_x(0)
    gs = [put(g, gv.at[:, col(k)], dev(k & 1, (k >> 1) & 1, k >> 2)) for k in range(1, 8)]
    g0 = load(g, gv.at[:, col(0)])
    w_yown(0)
    w_yown(1)
    ol = load(o.at[ds(mine, R, R), :], act.at[:, pl.ds(FP, HD // 2)])

    dc = [put(wd, dl.at[1, pl.ds(0, FP), :], CN), put(wo, dl.at[1, pl.ds(FP, HD // 2), :], CN)]
    qc0 = put(wq.at[:, ds(ix * QC, QC, QC)], ql.at[4], CN)

    x4.wait_recv()
    x5 = put(A.at[zr, col(4)], A.at[zr, col(5)], XN)
    zs = []

    def zput(p):
        zs.append(put(A.at[zr, col(p)], A.at[zr, col(p)], ZN))

    x1.wait_recv()
    zput(1)
    x2.wait_recv()
    x3 = put(A.at[zr, col(2)], A.at[zr, col(3)], XN)
    zput(2)
    x6.wait_recv()
    x7 = put(A.at[zr, col(6)], A.at[zr, col(7)], XN)
    zput(6)
    for j in range(1, PIECES):
        w_x(j)
    w_xgot(0)
    w_yown(2)
    x5.wait_recv()
    zput(5)
    x3.wait_recv()
    zput(3)
    x7.wait_recv()
    zput(7)
    for c in gs:
        c.wait_recv()
    g0.wait()
    x0.wait()
    for c in zs:
        c.wait_recv()

    def norm(row, n, gi):
        gain = gv[gi:gi + 1, :]

        def body(i, _):
            rows = ds(row + i * 32, 32, 32)
            v = A[rows, :].astype(F32)
            ss = jnp.sum(v * v, axis=-1, keepdims=True)
            N[rows, :] = (v * lax.rsqrt(ss / D + EPS) * gain).astype(BF)
            return 0

        lax.fori_loop(0, n // 32, body, 0)

    norm(0, R, 0)

    def gate_up(j):
        def body(t, _):
            rows = ds(lax.div(t, 2) * 256, 256, 256)
            c = lax.rem(t, 2) * 256
            n = N[rows, :]
            gt = _dot(n, W[wrow(j, 0, D), ds(c, 256, 256)])
            up = _dot(n, W[wrow(j, 0, D), ds(PC + c, 256, 256)])
            act[rows, ds(j * PC + c, 256, 256)] = (jax.nn.silu(gt) * up).astype(BF)
            return 0

        lax.fori_loop(0, (R // 256) * (PC // 256), body, 0)

    dy = {}

    def down_y(p):
        c = pl.ds(p * S, S)
        dy[p] = [put(wd.at[:, c], dl.at[0, pl.ds(0, FP), c], YN),
                 put(wo.at[:, c], dl.at[0, pl.ds(FP, HD // 2), c], YN)]

    acts = []
    for j in range(PIECES):
        if j + 1 < PIECES:
            w_xgot(j + 1)
        if j == 0:
            w_yown(3)
        if j == 2:
            for p in range(3):
                down_y(p)
        w_ygot(j)
        for c in wc[j]:
            c.wait_recv()
        gate_up(j)
        if j == 0:
            settle(zs + [x1, x2, x3, x4, x5, x6, x7] + gs)
        acts.append(put(act.at[:, pl.ds(j * PC, PC)], act.at[:, pl.ds(FP // 2 + j * PC, PC)], XN))

    qx = put(wq.at[:, ds((1 - ix) * QC, QC, QC)], ql.at[1], XN)
    qy = put(wq.at[:, ds(ix * QC, QC, QC)], ql.at[2], YN)

    for j in range(PIECES):
        settle(wx[j] + [wyo[j], wyf[j]] + wc[j])

    def down_load(ky, p):
        out = []
        for kc in range(2):
            c = pl.ds(p * S, S)
            if ky == 0 and kc == 0:
                top, bot = wd, wo.at[:, c]
            else:
                k = {(1, 0): 0, (0, 1): 1, (1, 1): 2}[ky, kc]
                top, bot = dl.at[k], dl.at[k, pl.ds(FP, HD // 2), c]
            to = pl.ds(p * 2 * S + kc * S, S)
            r0 = ky * K2
            out.append(load(top.at[ds(ix * (FP // 2), FP // 2, FP // 2), c], W.at[pl.ds(r0, FP // 2), to]))
            out.append(load(top.at[ds((1 - ix) * (FP // 2), FP // 2, FP // 2), c], W.at[pl.ds(r0 + FP // 2, FP // 2), to]))
            out.append(load(bot, W.at[pl.ds(r0 + FP, HD // 2), to]))
        return out

    for c in dc:
        c.wait_recv()
    dloads = {p: down_load(0, p) for p in range(3)}
    ol.wait()
    for c in acts:
        c.wait_recv()

    rs = {}

    def down(ky, p):
        s = (ky * 3 + p) * 2 * S
        w = lambda: W[pl.ds(ky * K2, K2), pl.ds(p * 2 * S, 2 * S)]

        def body(base, dst):
            def f(i, _):
                dst[ds(i * 256, 256, 256), pl.ds(s, 2 * S)] = _dot(act[ds(base + i * 256, 256, 256), :], w())
                return 0
            lax.fori_loop(0, Z // 256, f, 0)

        body((1 - z) * Z, ys)
        rs[ky, p] = put(ys.at[:, pl.ds(s, 2 * S)], yr.at[:, pl.ds(s, 2 * S)], ZN)
        body(z * Z, yo)

    def acol(ky, p, kc, kx=0):
        return pl.ds((2 * ky + 4 * kc + kx) * B + p * S, S)

    def finish(ky, p):
        rs[ky, p].wait_recv()

        def f(i, _):
            r = ds(i * 64, 64, 64)
            ra = ds(z * Z + i * 64, 64, 64)
            for kc in range(2):
                s = pl.ds((ky * 3 + p) * 2 * S + kc * S, S)
                c = acol(ky, p, kc)
                A[ra, c] = (A[ra, c].astype(F32) + (yo[r, s] + yr[r, s])).astype(BF)
            return 0

        lax.fori_loop(0, Z // 64, f, 0)

    xx, xz, xf = {}, {}, {}

    def share(ky, p):
        for kc in range(2):
            own, far = acol(ky, p, kc), acol(ky, p, kc, 1)
            xx[ky, p, kc] = put(A.at[zr, own], A.at[zr, far], XN)
            xz[ky, p, kc] = put(A.at[zr, own], A.at[zr, own], ZN)

    def forward(ky, p):
        for kc in range(2):
            own, far = acol(ky, p, kc), acol(ky, p, kc, 1)
            if ky == 0:
                xx[ky, p, kc].wait_recv()
                xf[ky, p, kc] = put(A.at[zr, far], A.at[zr, far], ZN)
            else:
                xz[ky, p, kc].wait_recv()
                xf[ky, p, kc] = put(A.at[zo, own], A.at[zo, far], XN)

    dyc = {}

    def down_ygot(p):
        for c in dy[p]:
            c.wait_recv()
        c = pl.ds(p * S, S)
        dyc[p] = put(dl.at[0, :, c], dl.at[2, :, c], CN)

    def down_ready(p):
        dyc[p].wait_recv()
        dloads[3 + p] = down_load(1, p)

    for p in range(3):
        for c in dloads[p]:
            c.wait()
        down(0, p)
    qx.wait_recv()
    qyf = put(ql.at[1], ql.at[3], YN)
    qc1 = put(ql.at[1], ql.at[5], CN)
    down_ygot(0)
    finish(0, 0)
    share(0, 0)
    down_ready(0)
    finish(0, 1)
    share(0, 1)
    forward(0, 0)
    for c in dloads[3]:
        c.wait()
    down(1, 0)
    finish(0, 2)
    share(0, 2)
    forward(0, 1)
    down_ygot(1)
    down_ready(1)
    finish(1, 0)
    share(1, 0)
    for c in dloads[4]:
        c.wait()
    down(1, 1)
    forward(0, 2)
    forward(1, 0)
    finish(1, 1)
    share(1, 1)
    down_ygot(2)
    down_ready(2)
    forward(1, 1)
    for c in dloads[5]:
        c.wait()
    down(1, 2)

    qy.wait_recv()
    qc2 = put(ql.at[2], ql.at[6], CN)
    finish(1, 2)
    share(1, 2)

    orow = ds(mine + z * Z, Z, Z)
    oy = put(A.at[zr, col(2)], xo.at[orow, :], YN)
    oyc = put(A.at[zr, col(6)], xo.at[orow, :], YCN)
    forward(1, 2)

    qyf.wait_recv()
    qc3 = put(ql.at[3], ql.at[7], CN)

    def qkv_load(k, src):
        return [load(src.at[:, pl.ds(0, 1024)], W.at[pl.ds(k * B, B), :]),
                load(src.at[:, pl.ds(1024, QC - 1024)], W.at[pl.ds(D + k * B, B), pl.ds(768, QC - 1024)])]

    qloads = []
    qloads += qkv_load(0, wq.at[:, ds(ix * QC, QC, QC)])
    for k in range(1, 4):
        qloads += qkv_load(k, ql.at[k])
    for k, c in zip(range(4, 8), (qc0, qc1, qc2, qc3)):
        c.wait_recv()
        qloads += qkv_load(k, ql.at[k])

    for p in range(3):
        for kc in range(2):
            xx[1, p, kc].wait_recv()
    for c in qloads:
        c.wait()
    settle(acts)

    xcol, ocol = ix * QC, (1 - ix) * QC
    qown, qxr, qyr, qdr, qcr = {}, {}, {}, {}, []

    def orows(py, pc, i):
        base = z * Z if i < 2 else (1 - z) * Z
        return ds(quarter(py, pc) + base + (i % 2) * CH, CH, CH)

    def at(rows, c):
        return qo.at[rows, ds(c, QC, QC)]

    def qkv_chunk(i):
        base = (z * Z if i < 2 else (1 - z) * Z) + (i % 2) * CH
        norm(base, CH, 1)
        rows = ds(base, CH, CH)

        def f(t, _):
            act[rows, ds(t * 256, 256, 256)] = _dot(N[rows, :], W[pl.ds(0, D), ds(t * 256, 256, 256)]).astype(BF)
            return 0

        lax.fori_loop(0, 4, f, 0)
        act[rows, pl.ds(1024, 256)] = _dot(N[rows, :], W[pl.ds(D, D), pl.ds(768, 256)]).astype(BF)
        src = act.at[rows, pl.ds(0, QC)]
        dst = at(orows(iy, ic, i), xcol)
        qxr[i] = put(src, dst, XN)
        qyr[i] = put(src, dst, YN)
        qcr.append(put(src, dst, CN))
        qown[i] = load(src, dst)

    qkv_chunk(0)
    qkv_chunk(1)
    for p in range(3):
        for kc in range(2):
            xz[0, p, kc].wait_recv()
            xf[0, p, kc].wait_recv()
            xf[1, p, kc].wait_recv()
    oc = put(A.at[:, col(4)], xo.at[ds(mine, R, R), :], CN)
    ol0 = load(A.at[:, col(0)], xo.at[ds(mine, R, R), :])
    oy.wait_recv()
    r0 = ds(quarter(1 - iy, ic) + z * Z, Z, Z)
    ozy = put(xo.at[r0, :], xo.at[r0, :], ZN)
    oyc.wait_recv()
    r1 = ds(quarter(1 - iy, 1 - ic) + z * Z, Z, Z)
    ozc = put(xo.at[r1, :], xo.at[r1, :], ZN)
    qkv_chunk(2)
    qkv_chunk(3)

    for i in range(4):
        qxr[i].wait_recv()
        ref = at(orows(iy, ic, i), ocol)
        if i % 2 == 0:
            qdr[i] = put(ref, ref, YN)
        qcr.append(put(ref, ref, CN))
        qyr[i].wait_recv()
        ref = at(orows(1 - iy, ic, i), xcol)
        if i % 2 == 1:
            qdr[i] = put(ref, ref, XN)
        qcr.append(put(ref, ref, CN))
    for i in range(4):
        qdr[i].wait_recv()
        ref = at(orows(1 - iy, ic, i), ocol)
        qcr.append(put(ref, ref, CN))
    for c in (oc, ozy, ozc):
        c.wait_recv()
    ol0.wait()
    for i in range(4):
        qown[i].wait()
    for c in qcr:
        c.wait_recv()
    settle(list(sends))


def solution(mesh):
    def body(x, g1, g2, w_gate, w_up, w_down, o, w_o, w_qkv):
        g = jnp.concatenate([g1[None], g2[None], jnp.zeros((6, B), F32)], 0)
        hbm = pl.BlockSpec(memory_space=pl.ANY)
        outs = pl.pallas_call(
            _kernel,
            out_shape=(jax.ShapeDtypeStruct((T, B), BF), jax.ShapeDtypeStruct((T, Q // 2), BF),
                       jax.ShapeDtypeStruct((3, K2, B), BF), jax.ShapeDtypeStruct((8, B, QC), BF)),
            in_specs=[hbm, pl.BlockSpec(memory_space=pltpu.VMEM)] + [hbm] * 6,
            out_specs=(hbm,) * 4,
            scratch_shapes=[
                pltpu.VMEM((R, D), BF), pltpu.VMEM((R, D), BF), pltpu.VMEM((PIECES * D, 2 * PC), BF),
                pltpu.VMEM((R, K2), BF), pltpu.VMEM((Z, 12 * S), F32), pltpu.VMEM((Z, 12 * S), F32),
                pltpu.VMEM((Z, 12 * S), F32), pltpu.VMEM((8, D), F32),
                pltpu.SemaphoreType.DMA((NREMOTE,)), pltpu.SemaphoreType.DMA((NREMOTE,)),
                pltpu.SemaphoreType.DMA((NLOCAL,)),
            ],
            compiler_params=pltpu.CompilerParams(collective_id=0, has_side_effects=True,
                                                 vmem_limit_bytes=67043328),
        )(x, g, w_gate, w_up, w_down, o, w_o, w_qkv)
        return outs[0], outs[1]

    in_specs = (P(None, 'h'), P('h'), P('h'), P('h', 'f'), P('h', 'f'), P('f', 'h'),
                P(None, 'f'), P('f', 'h'), P('h', 'f'))
    return jax.shard_map(body, mesh=mesh, in_specs=in_specs,
                         out_specs=(P(None, 'h'), P(None, 'f')), check_vma=False)
```

time: 2630 us -> 452 us (0.17)
  waiting for transfers between devices: 1610 us -> 0 us
  blocking collectives: 862 us -> 0 us
  Pallas kernels: 0 us -> 428 us
  matrix products: 136 us -> 0 us
    psum x3 -> x0, waiting for transfers between devices: 1610 us -> none  [the longest x2 1460 us: body(): gt, up = lax.psum((_dot(n, w_gate), _dot(n, w_up)), 'h')]
    psum x3 -> x0, blocking collectives: 862 us -> none  [the longest x1 812 us: body(): qkv = lax.psum(_dot(n1, w_qkv), 'h').astype(jnp.bfloat16)]
    pallas_call x0 -> x1, Pallas kernels: none -> 428 us  [body(): pl.pallas_call(_kernel, out_shape=(jax.ShapeDtypeStruct((T, B), BF), jax....]
    dot_general x5 -> x0, matrix products: 136 us -> none  [_dot(): return jnp.dot(a, b, preferred_element_type=jnp.float32)]
  transfers between devices with their start and end apart: 3 -> 0, of which waited for: 3 -> 0; matrix products, arithmetic and copies ran while one was open for 1% -> 0% of each run, Pallas kernels for 0% -> 0%
where the time goes in v1:
time: 452 us; the launch traced here: 451 us
  Pallas kernels  428 us (95%)
  local copies, waits for them, and re-layouts  22.5 us (5%)
    pallas_call x1, Pallas kernels, body(): pl.pallas_call(_kernel, out_shape=(jax.ShapeDtypeStruct((T, B), BF), jax....  428 us
    unnamed x2, local copies, waits for them, and re-layouts  21 us

profile of v1, /device:TPU:0, one launch (start us, length us, event | category | flops | bytes accessed | tf_op | source)
XLA Modules:
  0.0 451.5 jit_solution(14000711114228711875)
XLA Ops:
  0.6 0.1 pad.2.clone
  0.7 0.7 broadcast_in_dim.9
  1.4 0.7 broadcast_in_dim.10
  2.1 0.7 maximum_maximum_fusion.g
  2.8 427.7 %shard_map.104 = (bf16[4096,384]{1,0:T(8,128)(2,1)}, bf16[4096,2560]{1,0:T(8,128)(2,1)}, bf16[3,5632,384]{2,1,0:T(8,128)(2,1)}, bf16[8,384,1280]{2,1,0:T(8,128)(2,1)}) custom-call(bf16[4096,384]{1,0:T(8,128)(2,1)} %x.1, f32[8,384]{1,0:T(8,128)} %maximum_maximum_fusion.g, bf16[384,4096]{1,0:T(8,128)(2,1)} %wg.1, bf16[384,4096]{1,0:T(8,128)(2,1)} %wu.1, ...), custom_call_target="tpu_custom_call" | custom-call | tf_op jit(solution)/shard_map/pallas_call | solution.py:457
  430.5 3.9 copy.13
  434.3 17.2 %copy.14 = bf16[4096,2560]{1,0:T(8,128)(2,1)} copy(bf16[4096,2560]{1,0:T(8,128)(2,1)} %get-tuple-element.9) | data formatting | bytes 41943040
  (1 shorter events, 0.0 us)

commit v2 on v1

--- a/solution.py
+++ b/solution.py
@@ -8,7 +8,7 @@
 EPS = 1e-6
 BF, F32 = jnp.bfloat16, jnp.float32
 MESH = pl.DeviceIdType.MESH
-NREMOTE, NLOCAL = 176, 96
+NREMOTE, NLOCAL = 288, 128
 
 T, D, FF, HD, Q = 4096, 3072, 8192, 3072, 5120
 B = D // 8
@@ -20,7 +20,9 @@
 K2 = FP + HD // 2
 S = 128
 QC = Q // 4
-CH = 256
+QT = 256
+QG = ((0, 1), (1, 2), (3, 2))
+XFIRST = (2, 5, 8)
 
 
 def _dot(a, b):
@@ -181,9 +183,9 @@
 
     norm(0, R, 0)
 
-    def gate_up(j):
+    def gate_up(j, half):
         def body(t, _):
-            rows = ds(lax.div(t, 2) * 256, 256, 256)
+            rows = ds(half * Z + lax.div(t, 2) * 256, 256, 256)
             c = lax.rem(t, 2) * 256
             n = N[rows, :]
             gt = _dot(n, W[wrow(j, 0, D), ds(c, 256, 256)])
@@ -191,37 +193,14 @@
             act[rows, ds(j * PC + c, 256, 256)] = (jax.nn.silu(gt) * up).astype(BF)
             return 0
 
-        lax.fori_loop(0, (R // 256) * (PC // 256), body, 0)
-
-    dy = {}
+        lax.fori_loop(0, (Z // 256) * (PC // 256), body, 0)
+
+    dy, dyc, dloads = {}, {}, {}
 
     def down_y(p):
         c = pl.ds(p * S, S)
         dy[p] = [put(wd.at[:, c], dl.at[0, pl.ds(0, FP), c], YN),
                  put(wo.at[:, c], dl.at[0, pl.ds(FP, HD // 2), c], YN)]
-
-    acts = []
-    for j in range(PIECES):
-        if j + 1 < PIECES:
-            w_xgot(j + 1)
-        if j == 0:
-            w_yown(3)
-        if j == 2:
-            for p in range(3):
-                down_y(p)
-        w_ygot(j)
-        for c in wc[j]:
-            c.wait_recv()
-        gate_up(j)
-        if j == 0:
-            settle(zs + [x1, x2, x3, x4, x5, x6, x7] + gs)
-        acts.append(put(act.at[:, pl.ds(j * PC, PC)], act.at[:, pl.ds(FP // 2 + j * PC, PC)], XN))
-
-    qx = put(wq.at[:, ds((1 - ix) * QC, QC, QC)], ql.at[1], XN)
-    qy = put(wq.at[:, ds(ix * QC, QC, QC)], ql.at[2], YN)
-
-    for j in range(PIECES):
-        settle(wx[j] + [wyo[j], wyf[j]] + wc[j])
 
     def down_load(ky, p):
         out = []
@@ -237,33 +216,75 @@
             out.append(load(top.at[ds(ix * (FP // 2), FP // 2, FP // 2), c], W.at[pl.ds(r0, FP // 2), to]))
             out.append(load(top.at[ds((1 - ix) * (FP // 2), FP // 2, FP // 2), c], W.at[pl.ds(r0 + FP // 2, FP // 2), to]))
             out.append(load(bot, W.at[pl.ds(r0 + FP, HD // 2), to]))
-        return out
-
-    for c in dc:
-        c.wait_recv()
-    dloads = {p: down_load(0, p) for p in range(3)}
-    ol.wait()
-    for c in acts:
-        c.wait_recv()
+        dloads[ky, p] = out
+
+    def w_settle(j):
+        settle(wx[j] + [wyo[j], wyf[j]] + wc[j])
+
+    acts = {}
+
+    def act_put(j, half):
+        rows = zo if half else zr
+        acts[j, half] = put(act.at[rows, pl.ds(j * PC, PC)], act.at[rows, pl.ds(FP // 2 + j * PC, PC)], XN)
+
+    for j in range(PIECES):
+        if j + 1 < PIECES:
+            w_xgot(j + 1)
+        if j == 0:
+            w_yown(3)
+        if j == 2:
+            for p in range(3):
+                down_y(p)
+        if j == 3:
+            w_settle(0)
+            w_settle(1)
+            for c in dc:
+                c.wait_recv()
+            for p in range(3):
+                down_load(0, p)
+        w_ygot(j)
+        for c in wc[j]:
+            c.wait_recv()
+        gate_up(j, 1 - z)
+        if j == 0:
+            settle(zs + [x1, x2, x3, x4, x5, x6, x7] + gs)
+        act_put(j, 1)
+        if j == 3:
+            act_put(2, 0)
+        gate_up(j, z)
+        if j != 2:
+            act_put(j, 0)
+
+    qx = put(wq.at[:, ds((1 - ix) * QC, QC, QC)], ql.at[1], XN)
+    w_settle(2)
+    w_settle(3)
 
     rs = {}
 
-    def down(ky, p):
-        s = (ky * 3 + p) * 2 * S
-        w = lambda: W[pl.ds(ky * K2, K2), pl.ds(p * 2 * S, 2 * S)]
-
-        def body(base, dst):
-            def f(i, _):
-                dst[ds(i * 256, 256, 256), pl.ds(s, 2 * S)] = _dot(act[ds(base + i * 256, 256, 256), :], w())
-                return 0
-            lax.fori_loop(0, Z // 256, f, 0)
-
-        body((1 - z) * Z, ys)
-        rs[ky, p] = put(ys.at[:, pl.ds(s, 2 * S)], yr.at[:, pl.ds(s, 2 * S)], ZN)
-        body(z * Z, yo)
+    def step(ky, p):
+        return (ky * 3 + p) * 2 * S
+
+    def down(ky, p, half, dst):
+        def f(i, _):
+            w = W[pl.ds(ky * K2, K2), pl.ds(p * 2 * S, 2 * S)]
+            dst[ds(i * 256, 256, 256), pl.ds(step(ky, p), 2 * S)] = _dot(act[ds(half * Z + i * 256, 256, 256), :], w)
+            return 0
+        lax.fori_loop(0, Z // 256, f, 0)
+
+    def down_far(ky, p):
+        for c in dloads[ky, p]:
+            c.wait()
+        down(ky, p, 1 - z, ys)
+        s = pl.ds(step(ky, p), 2 * S)
+        rs[ky, p] = put(ys.at[:, s], yr.at[:, s], ZN)
+
+    def down_near(ky, p):
+        down(ky, p, z, yo)
 
     def acol(ky, p, kc, kx=0):
         return pl.ds((2 * ky + 4 * kc + kx) * B + p * S, S)
+
+    xx, xz, xf = {}, {}, {}
 
     def finish(ky, p):
         rs[ky, p].wait_recv()
@@ -272,32 +293,28 @@
             r = ds(i * 64, 64, 64)
             ra = ds(z * Z + i * 64, 64, 64)
             for kc in range(2):
-                s = pl.ds((ky * 3 + p) * 2 * S + kc * S, S)
+                s = pl.ds(step(ky, p) + kc * S, S)
                 c = acol(ky, p, kc)
                 A[ra, c] = (A[ra, c].astype(F32) + (yo[r, s] + yr[r, s])).astype(BF)
             return 0
 
         lax.fori_loop(0, Z // 64, f, 0)
-
-    xx, xz, xf = {}, {}, {}
-
-    def share(ky, p):
         for kc in range(2):
-            own, far = acol(ky, p, kc), acol(ky, p, kc, 1)
-            xx[ky, p, kc] = put(A.at[zr, own], A.at[zr, far], XN)
-            xz[ky, p, kc] = put(A.at[zr, own], A.at[zr, own], ZN)
-
-    def forward(ky, p):
+            xx[ky, p, kc] = put(A.at[zr, acol(ky, p, kc)], A.at[zr, acol(ky, p, kc, 1)], XN)
+
+    def z_own(ky, p):
         for kc in range(2):
-            own, far = acol(ky, p, kc), acol(ky, p, kc, 1)
-            if ky == 0:
-                xx[ky, p, kc].wait_recv()
-                xf[ky, p, kc] = put(A.at[zr, far], A.at[zr, far], ZN)
-            else:
-                xz[ky, p, kc].wait_recv()
-                xf[ky, p, kc] = put(A.at[zo, own], A.at[zo, far], XN)
-
-    dyc = {}
+            c = acol(ky, p, kc)
+            xz[ky, p, kc] = put(A.at[zr, c], A.at[zr, c], ZN)
+
+    def x_got(ky, p):
+        for kc in range(2):
+            xx[ky, p, kc].wait_recv()
+
+    def z_far(ky, p):
+        for kc in range(2):
+            c = acol(ky, p, kc, 1)
+            xf[ky, p, kc] = put(A.at[zr, c], A.at[zr, c], ZN)
 
     def down_ygot(p):
         for c in dy[p]:
@@ -307,113 +324,177 @@
 
     def down_ready(p):
         dyc[p].wait_recv()
-        dloads[3 + p] = down_load(1, p)
-
+        down_load(1, p)
+
+    ol.wait()
+    for j in range(PIECES):
+        acts[j, 1].wait_recv()
     for p in range(3):
-        for c in dloads[p]:
-            c.wait()
-        down(0, p)
+        down_far(0, p)
+    down_ygot(0)
+    down_ready(0)
+    down_far(1, 0)
+    for j in range(PIECES):
+        acts[j, 0].wait_recv()
+    for p in range(3):
+        down_near(0, p)
+    finish(0, 0)
+    finish(0, 1)
+    down_near(1, 0)
+    finish(0, 2)
+
+    qyo, qyf, qcy, qloads = {}, {}, {}, {}
+
+    def tile(t, n=1):
+        return pl.ds(t * QT, n * QT)
+
+    def qw_y(gi):
+        t, n = QG[gi]
+        qyo[gi] = put(wq.at[:, ds(ix * QC + t * QT, n * QT, QT)], ql.at[2, :, tile(t, n)], YN)
+        qyf[gi] = put(ql.at[1, :, tile(t, n)], ql.at[3, :, tile(t, n)], YN)
+
+    def qw_ygot(gi):
+        t, n = QG[gi]
+        qyo[gi].wait_recv()
+        a1 = put(ql.at[2, :, tile(t, n)], ql.at[6, :, tile(t, n)], CN)
+        qyf[gi].wait_recv()
+        a2 = put(ql.at[3, :, tile(t, n)], ql.at[7, :, tile(t, n)], CN)
+        qcy[gi] = (a1, a2)
+
+    def slot(t, k):
+        return W.at[pl.ds((D if t == 4 else 0) + k * B, B), pl.ds(3 * QT if t == 4 else t * QT, QT)]
+
+    def qload(gi, ks):
+        t0, n = QG[gi]
+        for t in range(t0, t0 + n):
+            for k in ks:
+                src = wq.at[:, ds(ix * QC + t * QT, QT, QT)] if k == 0 else ql.at[k, :, tile(t)]
+                qloads.setdefault(t, []).append(load(src, slot(t, k)))
+
     qx.wait_recv()
-    qyf = put(ql.at[1], ql.at[3], YN)
     qc1 = put(ql.at[1], ql.at[5], CN)
-    down_ygot(0)
-    finish(0, 0)
-    share(0, 0)
-    down_ready(0)
-    finish(0, 1)
-    share(0, 1)
-    forward(0, 0)
-    for c in dloads[3]:
-        c.wait()
-    down(1, 0)
-    finish(0, 2)
-    share(0, 2)
-    forward(0, 1)
+    for gi in range(len(QG)):
+        qw_y(gi)
+    qc0.wait_recv()
+    qc1.wait_recv()
+    for gi in range(len(QG)):
+        qload(gi, (0, 1, 4, 5))
+
     down_ygot(1)
     down_ready(1)
+    down_far(1, 1)
+    for p in range(3):
+        z_own(0, p)
     finish(1, 0)
-    share(1, 0)
-    for c in dloads[4]:
-        c.wait()
-    down(1, 1)
-    forward(0, 2)
-    forward(1, 0)
+    down_near(1, 1)
+    for p in range(3):
+        x_got(0, p)
     finish(1, 1)
-    share(1, 1)
     down_ygot(2)
     down_ready(2)
-    forward(1, 1)
-    for c in dloads[5]:
-        c.wait()
-    down(1, 2)
-
-    qy.wait_recv()
-    qc2 = put(ql.at[2], ql.at[6], CN)
+    down_far(1, 2)
+    for p in range(3):
+        z_far(0, p)
+    for p in range(2):
+        z_own(1, p)
+    for p in range(2):
+        x_got(1, p)
+        z_far(1, p)
+    down_near(1, 2)
+    settle([acts[k] for k in acts])
+    qw_ygot(0)
     finish(1, 2)
-    share(1, 2)
-
+    z_own(1, 2)
+    for c in qcy[0]:
+        c.wait_recv()
+    qload(0, (2, 3, 6, 7))
+    x_got(1, 2)
+    z_far(1, 2)
+    norm(z * Z, Z, 1)
+
+    qxr, qyr, qdr, qcr, qown = {}, {}, {}, [], []
+
+    def at(u, fy, fx):
+        half, t = (z if u < 5 else 1 - z), u % 5
+        py = 1 - iy if fy else iy
+        px = 1 - ix if fx else ix
+        return qo.at[ds(quarter(py, ic) + half * Z, Z, Z), ds(px * QC + t * QT, QT, QT)]
+
+    def unit(u):
+        t = u % 5
+        if u < 5:
+            for c in qloads[t]:
+                c.wait()
+        half = z if u < 5 else 1 - z
+
+        def f(i, _):
+            rows = ds(half * Z + i * 256, 256, 256)
+            w = W[pl.ds(D if t == 4 else 0, D), pl.ds(3 * QT if t == 4 else t * QT, QT)]
+            act[rows, pl.ds(t * QT, QT)] = _dot(N[rows, :], w).astype(BF)
+            return 0
+
+        lax.fori_loop(0, Z // 256, f, 0)
+        src, dst = act.at[ds(half * Z, Z, Z), pl.ds(t * QT, QT)], at(u, 0, 0)
+        qxr[u] = put(src, dst, XN)
+        qyr[u] = put(src, dst, YN)
+        qcr.append(put(src, dst, CN))
+        qown.append(load(src, dst))
+
+    def got_x(u):
+        qxr[u].wait_recv()
+        ref = at(u, 0, 1)
+        if u in XFIRST:
+            qdr[u] = put(ref, ref, YN)
+        qcr.append(put(ref, ref, CN))
+
+    def got_y(u):
+        qyr[u].wait_recv()
+        ref = at(u, 1, 0)
+        if u not in XFIRST:
+            qdr[u] = put(ref, ref, XN)
+        qcr.append(put(ref, ref, CN))
+
+    def got_d(u):
+        qdr[u].wait_recv()
+        ref = at(u, 1, 1)
+        qcr.append(put(ref, ref, CN))
+
+    unit(0)
+    qw_ygot(1)
+    for c in qcy[1]:
+        c.wait_recv()
+    qload(1, (2, 3, 6, 7))
+    unit(1)
+    unit(2)
+    got_x(0)
+    qw_ygot(2)
+    for c in qcy[2]:
+        c.wait_recv()
+    qload(2, (2, 3, 6, 7))
+    unit(3)
+    unit(4)
     orow = ds(mine + z * Z, Z, Z)
     oy = put(A.at[zr, col(2)], xo.at[orow, :], YN)
     oyc = put(A.at[zr, col(6)], xo.at[orow, :], YCN)
-    forward(1, 2)
-
-    qyf.wait_recv()
-    qc3 = put(ql.at[3], ql.at[7], CN)
-
-    def qkv_load(k, src):
-        return [load(src.at[:, pl.ds(0, 1024)], W.at[pl.ds(k * B, B), :]),
-                load(src.at[:, pl.ds(1024, QC - 1024)], W.at[pl.ds(D + k * B, B), pl.ds(768, QC - 1024)])]
-
-    qloads = []
-    qloads += qkv_load(0, wq.at[:, ds(ix * QC, QC, QC)])
-    for k in range(1, 4):
-        qloads += qkv_load(k, ql.at[k])
-    for k, c in zip(range(4, 8), (qc0, qc1, qc2, qc3)):
-        c.wait_recv()
-        qloads += qkv_load(k, ql.at[k])
-
-    for p in range(3):
-        for kc in range(2):
-            xx[1, p, kc].wait_recv()
-    for c in qloads:
-        c.wait()
-    settle(acts)
-
-    xcol, ocol = ix * QC, (1 - ix) * QC
-    qown, qxr, qyr, qdr, qcr = {}, {}, {}, {}, []
-
-    def orows(py, pc, i):
-        base = z * Z if i < 2 else (1 - z) * Z
-        return ds(quarter(py, pc) + base + (i % 2) * CH, CH, CH)
-
-    def at(rows, c):
-        return qo.at[rows, ds(c, QC, QC)]
-
-    def qkv_chunk(i):
-        base = (z * Z if i < 2 else (1 - z) * Z) + (i % 2) * CH
-        norm(base, CH, 1)
-        rows = ds(base, CH, CH)
-
-        def f(t, _):
-            act[rows, ds(t * 256, 256, 256)] = _dot(N[rows, :], W[pl.ds(0, D), ds(t * 256, 256, 256)]).astype(BF)
-            return 0
-
-        lax.fori_loop(0, 4, f, 0)
-        act[rows, pl.ds(1024, 256)] = _dot(N[rows, :], W[pl.ds(D, D), pl.ds(768, 256)]).astype(BF)
-        src = act.at[rows, pl.ds(0, QC)]
-        dst = at(orows(iy, ic, i), xcol)
-        qxr[i] = put(src, dst, XN)
-        qyr[i] = put(src, dst, YN)
-        qcr.append(put(src, dst, CN))
-        qown[i] = load(src, dst)
-
-    qkv_chunk(0)
-    qkv_chunk(1)
-    for p in range(3):
-        for kc in range(2):
-            xz[0, p, kc].wait_recv()
-            xf[0, p, kc].wait_recv()
-            xf[1, p, kc].wait_recv()
+    got_y(0)
+    got_x(1)
+    got_y(1)
+    got_x(2)
+    got_y(2)
+    for k in xz:
+        xz[k].wait_recv()
+    for k in xf:
+        xf[k].wait_recv()
+    norm((1 - z) * Z, Z, 1)
+    unit(5)
+    unit(6)
+    got_x(3)
+    got_y(3)
+    unit(7)
+    unit(8)
+    got_x(4)
+    got_y(4)
+    unit(9)
     oc = put(A.at[:, col(4)], xo.at[ds(mine, R, R), :], CN)
     ol0 = load(A.at[:, col(0)], xo.at[ds(mine, R, R), :])
     oy.wait_recv()
@@ -422,32 +503,36 @@
     oyc.wait_recv()
     r1 = ds(quarter(1 - iy, 1 - ic) + z * Z, Z, Z)
     ozc = put(xo.at[r1, :], xo.at[r1, :], ZN)
-    qkv_chunk(2)
-    qkv_chunk(3)
-
-    for i in range(4):
-        qxr[i].wait_recv()
-        ref = at(orows(iy, ic, i), ocol)
-        if i % 2 == 0:
-            qdr[i] = put(ref, ref, YN)
-        qcr.append(put(ref, ref, CN))
-        qyr[i].wait_recv()
-        ref = at(orows(1 - iy, ic, i), xcol)
-        if i % 2 == 1:
-            qdr[i] = put(ref, ref, XN)
-        qcr.append(put(ref, ref, CN))
-    for i in range(4):
-        qdr[i].wait_recv()
-        ref = at(orows(1 - iy, ic, i), ocol)
-        qcr.append(put(ref, ref, CN))
+    for u in range(5, 10):
+        got_x(u)
+        got_y(u)
+        got_d(u - 5)
+    for u in range(5, 10):
+        got_d(u)
     for c in (oc, ozy, ozc):
         c.wait_recv()
     ol0.wait()
-    for i in range(4):
-        qown[i].wait()
+    for c in qown:
+        c.wait()
     for c in qcr:
         c.wait_recv()
     settle(list(sends))
+
+
+def _copy(a, b, ao, bo):
+    ao[...] = a[...]
+    bo[...] = b[...]
+
+
+def _hand_over(a, b, rows=512):
+    spec = lambda v: pl.BlockSpec((rows, v.shape[1]), lambda i: (i, 0))
+    return pl.pallas_call(
+        _copy,
+        grid=(a.shape[0] // rows,),
+        out_shape=(jax.ShapeDtypeStruct(a.shape, a.dtype), jax.ShapeDtypeStruct(b.shape, b.dtype)),
+        in_specs=[spec(a), spec(b)],
+        out_specs=(spec(a), spec(b)),
+    )(a, b)
 
 
 def solution(mesh):
@@ -470,7 +555,7 @@
             compiler_params=pltpu.CompilerParams(collective_id=0, has_side_effects=True,
                                                  vmem_limit_bytes=67043328),
         )(x, g, w_gate, w_up, w_down, o, w_o, w_qkv)
-        return outs[0], outs[1]
+        return _hand_over(outs[0], outs[1])
 
     in_specs = (P(None, 'h'), P('h'), P('h'), P('h', 'f'), P('h', 'f'), P('f', 'h'),
                 P(None, 'f'), P('f', 'h'), P('h', 'f'))

time: 452 us -> 414 us (0.916)
  local copies, waits for them, and re-layouts: 22.5 us -> 1.44 us
  Pallas kernels: 428 us -> 411 us
    pallas_call x1, Pallas kernels: 428 us -> 393 us  [body(): pl.pallas_call(_kernel, out_shape=(jax.ShapeDtypeStruct((T, B), BF), jax....]
    unnamed x2 -> x0, local copies, waits for them, and re-layouts: 21 us -> none
    pallas_call x0 -> x1, Pallas kernels: none -> 17.9 us  [_hand_over(): pl.pallas_call(_copy, grid=(a.shape[0] // rows,), out_shape=(jax.ShapeDty...]
where the time goes in v2:
time: 414 us
  Pallas kernels  411 us (99%)
    pallas_call x1, Pallas kernels, body(): pl.pallas_call(_kernel, out_shape=(jax.ShapeDtypeStruct((T, B), BF), jax....  393 us
    pallas_call x1, Pallas kernels, _hand_over(): pl.pallas_call(_copy, grid=(a.shape[0] // rows,), out_shape=(jax.ShapeDty...  17.9 us

profile of v2, /device:TPU:0, one launch (start us, length us, event | category | flops | bytes accessed | tf_op | source)
XLA Modules:
  0.0 413.8 jit_solution(1433142455364145430)
XLA Ops:
  0.6 0.1 pad.2.clone
  0.7 0.7 broadcast_in_dim.9
  1.4 0.7 broadcast_in_dim.10
  2.1 0.7 maximum_maximum_fusion.g
  2.8 393.2 %shard_map.104 = (bf16[4096,384]{1,0:T(8,128)(2,1)}, bf16[4096,2560]{1,0:T(8,128)(2,1)}, bf16[3,5632,384]{2,1,0:T(8,128)(2,1)}, bf16[8,384,1280]{2,1,0:T(8,128)(2,1)}) custom-call(bf16[4096,384]{1,0:T(8,128)(2,1)} %x.1, f32[8,384]{1,0:T(8,128)} %maximum_maximum_fusion.g, bf16[384,4096]{1,0:T(8,128)(2,1)} %wg.1, bf16[384,4096]{1,0:T(8,128)(2,1)} %wu.1, ...), custom_call_target="tpu_custom_call" | custom-call | tf_op jit(solution)/shard_map/pallas_call | solution.py:542
  395.9 17.9 %shard_map.105 = (bf16[4096,384]{1,0:T(8,128)(2,1)}, bf16[4096,2560]{1,0:T(8,128)(2,1)}) custom-call(bf16[4096,384]{1,0:T(8,128)(2,1)} %get-tuple-element.4.a, bf16[4096,2560]{1,0:T(8,128)(2,1)} %get-tuple-element.5.b), custom_call_target="tpu_custom_call" | custom-call | tf_op jit(solution)/shard_map/pallas_call | solution.py:529
  (1 shorter events, 0.0 us)

commit v3 on v2

--- a/solution.py
+++ b/solution.py
@@ -22,6 +22,8 @@
 QC = Q // 4
 QT = 256
 QG = ((0, 1), (1, 2), (3, 2))
+QSLOT = ((0, 512), (D, 512), (0, 768), (D, 768), (0, 0))
+VMEM_LIMIT = 67043328 - T * (B + Q // 2) * 2 - 65536
 XFIRST = (2, 5, 8)
 
 
@@ -29,7 +31,7 @@
     return jnp.dot(a, b, preferred_element_type=F32)
 
 
-def _kernel(x, g, wg, wu, wd, o, wo, wq, xo, qo, dl, ql,
+def _kernel(x, g, wg, wu, wd, o, wo, wq, xo, qo, dl, ql, wh,
             A, N, W, act, ys, yr, yo, gv, send, recv, loc):
     h = lax.axis_index('h')
     z = lax.axis_index('f')
@@ -94,45 +96,75 @@
     x0 = load(x.at[ds(mine, R, R), :], A.at[:, col(0)])
 
     def wrow(j, a, n):
-        return pl.ds(j * D + a, n)
+        return pl.ds((j % 2) * D + a, n)
+
+    def wref(j, a, n, c=slice(None)):
+        return W.at[wrow(j, a, n), c] if j < 2 else wh.at[j - 2, pl.ds(a, n), c]
 
     wl, wx, wyo, wyf, wc = {}, {}, {}, {}, {}
+    GC, UC = pl.ds(0, PC), pl.ds(PC, PC)
+
+    def wcol(j, other):
+        return ds(((1 - ix) if other else ix) * (FP // 2) + j * PC, PC, PC)
 
     def w_load(j):
-        c0 = ds(ix * (FP // 2) + j * PC, PC, PC)
-        wl[j] = [load(wg.at[:, c0], W.at[wrow(j, 0, B), pl.ds(0, PC)]),
-                 load(wu.at[:, c0], W.at[wrow(j, 0, B), pl.ds(PC, PC)])]
+        c0 = wcol(j, 0)
+        wl[j] = [load(wg.at[:, c0], W.at[wrow(j, 0, B), GC]), load(wu.at[:, c0], W.at[wrow(j, 0, B), UC])]
 
     def w_x(j):
-        c1 = ds((1 - ix) * (FP // 2) + j * PC, PC, PC)
-        wx[j] = [put(wg.at[:, c1], W.at[wrow(j, B, B), pl.ds(0, PC)], XN),
-                 put(wu.at[:, c1], W.at[wrow(j, B, B), pl.ds(PC, PC)], XN)]
+        c1 = wcol(j, 1)
+        wx[j] = [put(wg.at[:, c1], wref(j, B, B, GC), XN), put(wu.at[:, c1], wref(j, B, B, UC), XN)]
 
     def w_yown(j):
-        for c in wl[j]:
-            c.wait()
-        wyo[j] = put(W.at[wrow(j, 0, B), :], W.at[wrow(j, 2 * B, B), :], YN)
+        if j < 2:
+            for c in wl[j]:
+                c.wait()
+            wyo[j] = [put(wref(j, 0, B), wref(j, 2 * B, B), YN)]
+            wc[j] = [put(wref(j, 0, B), wref(j, 4 * B, B), CN)]
+        else:
+            c0 = wcol(j, 0)
+            wyo[j] = [put(wg.at[:, c0], wref(j, 2 * B, B, GC), YN), put(wu.at[:, c0], wref(j, 2 * B, B, UC), YN)]
+            wc[j] = [put(wg.at[:, c0], wref(j, 4 * B, B, GC), CN), put(wu.at[:, c0], wref(j, 4 * B, B, UC), CN)]
 
     def w_xgot(j):
         for c in wx[j]:
             c.wait_recv()
-        wyf[j] = put(W.at[wrow(j, B, B), :], W.at[wrow(j, 3 * B, B), :], YN)
-        wc[j] = [put(W.at[wrow(j, 0, 2 * B), :], W.at[wrow(j, 4 * B, 2 * B), :], CN)]
+        wyf[j] = [put(wref(j, B, B), wref(j, 3 * B, B), YN)]
+        wc[j].append(put(wref(j, B, B), wref(j, 5 * B, B), CN))
+
+    def w_block(j, k, n=1):
+        return load(wref(j, k * B, n * B), W.at[wrow(j, k * B, n * B), :])
 
     def w_ygot(j):
-        wyo[j].wait_recv()
-        wc[j].append(put(W.at[wrow(j, 2 * B, B), :], W.at[wrow(j, 6 * B, B), :], CN))
-        wyf[j].wait_recv()
-        wc[j].append(put(W.at[wrow(j, 3 * B, B), :], W.at[wrow(j, 7 * B, B), :], CN))
-
-    for j in range(PIECES):
-        w_load(j)
+        for c in wyo[j]:
+            c.wait_recv()
+        own = len(wc[j])
+        wc[j].append(put(wref(j, 2 * B, B), wref(j, 6 * B, B), CN))
+        loads = []
+        if j >= 2:
+            w_load(j)
+            for c in wc[j][:own]:
+                c.wait_recv()
+            loads = wl[j] + [w_block(j, 1, 2), w_block(j, 4, 2)]
+        for c in wyf[j]:
+            c.wait_recv()
+        wc[j].append(put(wref(j, 3 * B, B), wref(j, 7 * B, B), CN))
+        if j >= 2:
+            loads.append(w_block(j, 3))
+        for c in wc[j] if j < 2 else wc[j][own:]:
+            c.wait_recv()
+        if j >= 2:
+            loads.append(w_block(j, 6, 2))
+        for c in loads:
+            c.wait()
+
+    w_load(0)
+    w_load(1)
     w_x(0)
     gs = [put(g, gv.at[:, col(k)], dev(k & 1, (k >> 1) & 1, k >> 2)) for k in range(1, 8)]
     g0 = load(g, gv.at[:, col(0)])
     w_yown(0)
     w_yown(1)
-    ol = load(o.at[ds(mine, R, R), :], act.at[:, pl.ds(FP, HD // 2)])
 
     dc = [put(wd, dl.at[1, pl.ds(0, FP), :], CN), put(wo, dl.at[1, pl.ds(FP, HD // 2), :], CN)]
     qc0 = put(wq.at[:, ds(ix * QC, QC, QC)], ql.at[4], CN)
@@ -202,6 +234,9 @@
         dy[p] = [put(wd.at[:, c], dl.at[0, pl.ds(0, FP), c], YN),
                  put(wo.at[:, c], dl.at[0, pl.ds(FP, HD // 2), c], YN)]
 
+    def dslot(ky, p):
+        return ((ky * 3 + p) % 4) * 2 * S
+
     def down_load(ky, p):
         out = []
         for kc in range(2):
@@ -211,15 +246,14 @@
             else:
                 k = {(1, 0): 0, (0, 1): 1, (1, 1): 2}[ky, kc]
                 top, bot = dl.at[k], dl.at[k, pl.ds(FP, HD // 2), c]
-            to = pl.ds(p * 2 * S + kc * S, S)
-            r0 = ky * K2
-            out.append(load(top.at[ds(ix * (FP // 2), FP // 2, FP // 2), c], W.at[pl.ds(r0, FP // 2), to]))
-            out.append(load(top.at[ds((1 - ix) * (FP // 2), FP // 2, FP // 2), c], W.at[pl.ds(r0 + FP // 2, FP // 2), to]))
-            out.append(load(bot, W.at[pl.ds(r0 + FP, HD // 2), to]))
+            to = pl.ds(dslot(ky, p) + kc * S, S)
+            out.append(load(top.at[ds(ix * (FP // 2), FP // 2, FP // 2), c], W.at[pl.ds(0, FP // 2), to]))
+            out.append(load(top.at[ds((1 - ix) * (FP // 2), FP // 2, FP // 2), c], W.at[pl.ds(FP // 2, FP // 2), to]))
+            out.append(load(bot, W.at[pl.ds(FP, HD // 2), to]))
         dloads[ky, p] = out
 
     def w_settle(j):
-        settle(wx[j] + [wyo[j], wyf[j]] + wc[j])
+        settle(wx[j] + wyo[j] + wyf[j] + wc[j])
 
     acts = {}
 
@@ -233,18 +267,12 @@
         if j == 0:
             w_yown(3)
         if j == 2:
+            w_settle(0)
             for p in range(3):
                 down_y(p)
         if j == 3:
-            w_settle(0)
             w_settle(1)
-            for c in dc:
-                c.wait_recv()
-            for p in range(3):
-                down_load(0, p)
         w_ygot(j)
-        for c in wc[j]:
-            c.wait_recv()
         gate_up(j, 1 - z)
         if j == 0:
             settle(zs + [x1, x2, x3, x4, x5, x6, x7] + gs)
@@ -256,30 +284,42 @@
             act_put(j, 0)
 
     qx = put(wq.at[:, ds((1 - ix) * QC, QC, QC)], ql.at[1], XN)
-    w_settle(2)
-    w_settle(3)
+    for c in dc:
+        c.wait_recv()
+    for p in range(3):
+        down_load(0, p)
+    ol = load(o.at[ds(mine, R, R), :], N.at[:, pl.ds(0, HD // 2)])
 
     rs = {}
 
     def step(ky, p):
         return (ky * 3 + p) * 2 * S
 
-    def down(ky, p, half, dst):
+    def down(ky, p, half, dst, at, i0=0, n=Z // 256):
         def f(i, _):
-            w = W[pl.ds(ky * K2, K2), pl.ds(p * 2 * S, 2 * S)]
-            dst[ds(i * 256, 256, 256), pl.ds(step(ky, p), 2 * S)] = _dot(act[ds(half * Z + i * 256, 256, 256), :], w)
+            c = pl.ds(dslot(ky, p), 2 * S)
+            rows = ds(half * Z + i * 256, 256, 256)
+            dst[ds(i * 256, 256, 256), pl.ds(at, 2 * S)] = (
+                _dot(act[rows, :], W[pl.ds(0, FP), c]) + _dot(N[rows, pl.ds(0, HD // 2)], W[pl.ds(FP, HD // 2), c]))
             return 0
-        lax.fori_loop(0, Z // 256, f, 0)
+        lax.fori_loop(i0, i0 + n, f, 0)
+
+    def parts(ky, p):
+        return ((0, 256), (256, 256)) if (ky, p) == (1, 2) else ((0, Z),)
 
     def down_far(ky, p):
         for c in dloads[ky, p]:
             c.wait()
-        down(ky, p, 1 - z, ys)
         s = pl.ds(step(ky, p), 2 * S)
-        rs[ky, p] = put(ys.at[:, s], yr.at[:, s], ZN)
+        for r, n in parts(ky, p):
+            down(ky, p, 1 - z, ys, step(ky, p), r // 256, n // 256)
+            rs[ky, p, r] = put(ys.at[pl.ds(r, n), s], yr.at[pl.ds(r, n), s], ZN)
+
+    def near(ky, p):
+        return ((ky * 3 + p) % 2) * 2 * S
 
     def down_near(ky, p):
-        down(ky, p, z, yo)
+        down(ky, p, z, yo, near(ky, p))
 
     def acol(ky, p, kc, kx=0):
         return pl.ds((2 * ky + 4 * kc + kx) * B + p * S, S)
@@ -287,20 +327,22 @@
     xx, xz, xf = {}, {}, {}
 
     def finish(ky, p):
-        rs[ky, p].wait_recv()
-
-        def f(i, _):
-            r = ds(i * 64, 64, 64)
-            ra = ds(z * Z + i * 64, 64, 64)
+        for r0, n in parts(ky, p):
+            rs[ky, p, r0].wait_recv()
+
+            def f(i, _):
+                r = ds(r0 + i * 64, 64, 64)
+                ra = ds(z * Z + r0 + i * 64, 64, 64)
+                for kc in range(2):
+                    c = acol(ky, p, kc)
+                    mine_y = yo[r, pl.ds(near(ky, p) + kc * S, S)]
+                    A[ra, c] = (A[ra, c].astype(F32) + (mine_y + yr[r, pl.ds(step(ky, p) + kc * S, S)])).astype(BF)
+                return 0
+
+            lax.fori_loop(0, n // 64, f, 0)
+            rows = ds(z * Z + r0, n, n)
             for kc in range(2):
-                s = pl.ds(step(ky, p) + kc * S, S)
-                c = acol(ky, p, kc)
-                A[ra, c] = (A[ra, c].astype(F32) + (yo[r, s] + yr[r, s])).astype(BF)
-            return 0
-
-        lax.fori_loop(0, Z // 64, f, 0)
-        for kc in range(2):
-            xx[ky, p, kc] = put(A.at[zr, acol(ky, p, kc)], A.at[zr, acol(ky, p, kc, 1)], XN)
+                xx[ky, p, kc, r0] = put(A.at[rows, acol(ky, p, kc)], A.at[rows, acol(ky, p, kc, 1)], XN)
 
     def z_own(ky, p):
         for kc in range(2):
@@ -308,8 +350,9 @@
             xz[ky, p, kc] = put(A.at[zr, c], A.at[zr, c], ZN)
 
     def x_got(ky, p):
-        for kc in range(2):
-            xx[ky, p, kc].wait_recv()
+        for r0, _ in parts(ky, p):
+            for kc in range(2):
+                xx[ky, p, kc, r0].wait_recv()
 
     def z_far(ky, p):
         for kc in range(2):
@@ -336,9 +379,10 @@
     down_far(1, 0)
     for j in range(PIECES):
         acts[j, 0].wait_recv()
-    for p in range(3):
-        down_near(0, p)
+    down_near(0, 0)
+    down_near(0, 1)
     finish(0, 0)
+    down_near(0, 2)
     finish(0, 1)
     down_near(1, 0)
     finish(0, 2)
@@ -362,7 +406,8 @@
         qcy[gi] = (a1, a2)
 
     def slot(t, k):
-        return W.at[pl.ds((D if t == 4 else 0) + k * B, B), pl.ds(3 * QT if t == 4 else t * QT, QT)]
+        r, c = QSLOT[t]
+        return W.at[pl.ds(r + k * B, B), pl.ds(c, QT)]
 
     def qload(gi, ks):
         t0, n = QG[gi]
@@ -377,7 +422,7 @@
         qw_y(gi)
     qc0.wait_recv()
     qc1.wait_recv()
-    for gi in range(len(QG)):
+    for gi in range(2):
         qload(gi, (0, 1, 4, 5))
 
     down_ygot(1)
@@ -387,6 +432,7 @@
         z_own(0, p)
     finish(1, 0)
     down_near(1, 1)
+    qload(2, (0, 1, 4, 5))
     for p in range(3):
         x_got(0, p)
     finish(1, 1)
@@ -401,7 +447,6 @@
         x_got(1, p)
         z_far(1, p)
     down_near(1, 2)
-    settle([acts[k] for k in acts])
     qw_ygot(0)
     finish(1, 2)
     z_own(1, 2)
@@ -412,7 +457,7 @@
     z_far(1, 2)
     norm(z * Z, Z, 1)
 
-    qxr, qyr, qdr, qcr, qown = {}, {}, {}, [], []
+    qxr, qyr, qdr, qcr = {}, {}, {}, []
 
     def at(u, fy, fx):
         half, t = (z if u < 5 else 1 - z), u % 5
@@ -428,17 +473,17 @@
         half = z if u < 5 else 1 - z
 
         def f(i, _):
-            rows = ds(half * Z + i * 256, 256, 256)
-            w = W[pl.ds(D if t == 4 else 0, D), pl.ds(3 * QT if t == 4 else t * QT, QT)]
-            act[rows, pl.ds(t * QT, QT)] = _dot(N[rows, :], w).astype(BF)
+            r, c = QSLOT[t]
+            w = W[pl.ds(r, D), pl.ds(c, QT)]
+            to = qo.at[ds(mine + half * Z + i * 256, 256, 256), ds(ix * QC + t * QT, QT, QT)]
+            to[...] = _dot(N[ds(half * Z + i * 256, 256, 256), :], w).astype(BF)
             return 0
 
         lax.fori_loop(0, Z // 256, f, 0)
-        src, dst = act.at[ds(half * Z, Z, Z), pl.ds(t * QT, QT)], at(u, 0, 0)
-        qxr[u] = put(src, dst, XN)
-        qyr[u] = put(src, dst, YN)
-        qcr.append(put(src, dst, CN))
-        qown.append(load(src, dst))
+        ref = at(u, 0, 0)
+        qxr[u] = put(ref, ref, XN)
+        qyr[u] = put(ref, ref, YN)
+        qcr.append(put(ref, ref, CN))
 
     def got_x(u):
         qxr[u].wait_recv()
@@ -496,7 +541,12 @@
     got_y(4)
     unit(9)
     oc = put(A.at[:, col(4)], xo.at[ds(mine, R, R), :], CN)
-    ol0 = load(A.at[:, col(0)], xo.at[ds(mine, R, R), :])
+
+    def keep(i, _):
+        xo[ds(mine + i * 128, 128, 128), :] = A[ds(i * 128, 128, 128), col(0)]
+        return 0
+
+    lax.fori_loop(0, R // 128, keep, 0)
     oy.wait_recv()
     r0 = ds(quarter(1 - iy, ic) + z * Z, Z, Z)
     ozy = put(xo.at[r0, :], xo.at[r0, :], ZN)
@@ -511,51 +561,34 @@
         got_d(u)
     for c in (oc, ozy, ozc):
         c.wait_recv()
-    ol0.wait()
-    for c in qown:
-        c.wait()
     for c in qcr:
         c.wait_recv()
     settle(list(sends))
-
-
-def _copy(a, b, ao, bo):
-    ao[...] = a[...]
-    bo[...] = b[...]
-
-
-def _hand_over(a, b, rows=512):
-    spec = lambda v: pl.BlockSpec((rows, v.shape[1]), lambda i: (i, 0))
-    return pl.pallas_call(
-        _copy,
-        grid=(a.shape[0] // rows,),
-        out_shape=(jax.ShapeDtypeStruct(a.shape, a.dtype), jax.ShapeDtypeStruct(b.shape, b.dtype)),
-        in_specs=[spec(a), spec(b)],
-        out_specs=(spec(a), spec(b)),
-    )(a, b)
 
 
 def solution(mesh):
     def body(x, g1, g2, w_gate, w_up, w_down, o, w_o, w_qkv):
-        g = jnp.concatenate([g1[None], g2[None], jnp.zeros((6, B), F32)], 0)
-        hbm = pl.BlockSpec(memory_space=pl.ANY)
+        spread = lambda v: lax.broadcast_in_dim(v, (8, B), (1,))
+        g = jnp.where(lax.broadcasted_iota(jnp.int32, (8, B), 0) == 0, spread(g1), spread(g2))
+        hbm, vmem = pl.BlockSpec(memory_space=pltpu.HBM), pl.BlockSpec(memory_space=pltpu.VMEM)
+        keep = lambda v: pltpu.with_memory_space_constraint(v, pltpu.HBM)
         outs = pl.pallas_call(
             _kernel,
-            out_shape=(jax.ShapeDtypeStruct((T, B), BF), jax.ShapeDtypeStruct((T, Q // 2), BF),
-                       jax.ShapeDtypeStruct((3, K2, B), BF), jax.ShapeDtypeStruct((8, B, QC), BF)),
-            in_specs=[hbm, pl.BlockSpec(memory_space=pltpu.VMEM)] + [hbm] * 6,
-            out_specs=(hbm,) * 4,
+            out_shape=(pltpu.VMEM((T, B), BF), pltpu.VMEM((T, Q // 2), BF), pltpu.HBM((3, K2, B), BF),
+                       pltpu.HBM((8, B, QC), BF), pltpu.HBM((2, D, 2 * PC), BF)),
+            in_specs=[hbm, vmem] + [hbm] * 6,
+            out_specs=(vmem, vmem, hbm, hbm, hbm),
             scratch_shapes=[
-                pltpu.VMEM((R, D), BF), pltpu.VMEM((R, D), BF), pltpu.VMEM((PIECES * D, 2 * PC), BF),
-                pltpu.VMEM((R, K2), BF), pltpu.VMEM((Z, 12 * S), F32), pltpu.VMEM((Z, 12 * S), F32),
-                pltpu.VMEM((Z, 12 * S), F32), pltpu.VMEM((8, D), F32),
+                pltpu.VMEM((R, D), BF), pltpu.VMEM((R, D), BF), pltpu.VMEM((2 * D, 2 * PC), BF),
+                pltpu.VMEM((R, FP), BF), pltpu.VMEM((Z, 12 * S), F32), pltpu.VMEM((Z, 12 * S), F32),
+                pltpu.VMEM((Z, 4 * S), F32), pltpu.VMEM((8, D), F32),
                 pltpu.SemaphoreType.DMA((NREMOTE,)), pltpu.SemaphoreType.DMA((NREMOTE,)),
                 pltpu.SemaphoreType.DMA((NLOCAL,)),
             ],
             compiler_params=pltpu.CompilerParams(collective_id=0, has_side_effects=True,
-                                                 vmem_limit_bytes=67043328),
-        )(x, g, w_gate, w_up, w_down, o, w_o, w_qkv)
-        return _hand_over(outs[0], outs[1])
+                                                 vmem_limit_bytes=VMEM_LIMIT),
+        )(keep(x), g, *[keep(v) for v in (w_gate, w_up, w_down, o, w_o, w_qkv)])
+        return outs[0], outs[1]
 
     in_specs = (P(None, 'h'), P('h'), P('h'), P('h', 'f'), P('h', 'f'), P('f', 'h'),
                 P(None, 'f'), P('f', 'h'), P('h', 'f'))

time: 414 us -> 406 us (0.981)
  Pallas kernels: 411 us -> 394 us
  local copies, waits for them, and re-layouts: 1.44 us -> 9.21 us
    pallas_call x2 -> x1, Pallas kernels: 411 us -> 394 us  [body(): pl.pallas_call(_kernel, out_shape=(pltpu.VMEM((T, B), BF), pltpu.VMEM((T,...]
    unnamed x0 -> x2, local copies, waits for them, and re-layouts: none -> 9.21 us
where the time goes in v3:
time: 406 us
  Pallas kernels  394 us (97%)
  local copies, waits for them, and re-layouts  9.21 us (2%)
    pallas_call x1, Pallas kernels, body(): pl.pallas_call(_kernel, out_shape=(pltpu.VMEM((T, B), BF), pltpu.VMEM((T,...  394 us
    unnamed x2, local copies, waits for them, and re-layouts  9.21 us

profile of v3, /device:TPU:0, one launch (start us, length us, event | category | flops | bytes accessed | tf_op | source)
XLA Modules:
  0.0 405.5 jit_solution(6530802568697426463)
XLA Ops:
  0.6 1.4 broadcast_select_fusion.g
  2.0 394.3 %shard_map.104 = (bf16[4096,384]{1,0:T(8,128)(2,1)S(1)}, bf16[4096,2560]{1,0:T(8,128)(2,1)S(1)}, bf16[3,5632,384]{2,1,0:T(8,128)(2,1)}, bf16[8,384,1280]{2,1,0:T(8,128)(2,1)}, bf16[2,3072,1024]{2,1,0:T(8,128)(2,1)}) custom-call(bf16[4096,384]{1,0:T(8,128)(2,1)} %x.1, f32[8,384]{1,0:T(8,128)} %broadcast_select_fusion.g, bf16[384,4096]{1,0:T(8,128)(2,1)} %wg.1, ...), custom_call_target="tpu_custom_call" | custom-call | tf_op jit(solution)/shard_map/pallas_call | solution.py:575
  396.3 1.7 copy.13
  398.0 7.5 %copy.14 = bf16[4096,2560]{1,0:T(8,128)(2,1)} copy(bf16[4096,2560]{1,0:T(8,128)(2,1)S(1)} %get-tuple-element.7) | data formatting | bytes 41943040
  (1 shorter events, 0.0 us)

commit v4 on v3

--- a/solution.py
+++ b/solution.py
@@ -20,11 +20,16 @@
 K2 = FP + HD // 2
 S = 128
 QC = Q // 4
+M = 256
+FX, OC, S2 = FP // 2, HD // 2, 2 * S
 QT = 256
-QG = ((0, 1), (1, 2), (3, 2))
+QN = QC // QT
+EARLY, LATE = (0, 1, 4, 5), (2, 3, 6, 7)
 QSLOT = ((0, 512), (D, 512), (0, 768), (D, 768), (0, 0))
 VMEM_LIMIT = 67043328 - T * (B + Q // 2) * 2 - 65536
-XFIRST = (2, 5, 8)
+UNITS = ((0, 0, M, 0), (0, M, M, 0)) + tuple((0, 0, Z, t) for t in range(1, 5)) + (
+    tuple((1, 0, Z, t) for t in range(4)) + ((1, 0, M, 4), (1, M, M, 4)))
+XFIRST = (3, 7)
 
 
 def _dot(a, b):
@@ -105,7 +110,7 @@
     GC, UC = pl.ds(0, PC), pl.ds(PC, PC)
 
     def wcol(j, other):
-        return ds(((1 - ix) if other else ix) * (FP // 2) + j * PC, PC, PC)
+        return ds(((1 - ix) if other else ix) * FX + j * PC, PC, PC)
 
     def w_load(j):
         c0 = wcol(j, 0)
@@ -166,7 +171,7 @@
     w_yown(0)
     w_yown(1)
 
-    dc = [put(wd, dl.at[1, pl.ds(0, FP), :], CN), put(wo, dl.at[1, pl.ds(FP, HD // 2), :], CN)]
+    dc = [put(wd, dl.at[1, pl.ds(0, FP), :], CN), put(wo, dl.at[1, pl.ds(FP, OC), :], CN)]
     qc0 = put(wq.at[:, ds(ix * QC, QC, QC)], ql.at[4], CN)
 
     x4.wait_recv()
@@ -217,25 +222,25 @@
 
     def gate_up(j, half):
         def body(t, _):
-            rows = ds(half * Z + lax.div(t, 2) * 256, 256, 256)
-            c = lax.rem(t, 2) * 256
+            rows = ds(half * Z + lax.div(t, 2) * M, M, M)
+            c = lax.rem(t, 2) * M
             n = N[rows, :]
-            gt = _dot(n, W[wrow(j, 0, D), ds(c, 256, 256)])
-            up = _dot(n, W[wrow(j, 0, D), ds(PC + c, 256, 256)])
-            act[rows, ds(j * PC + c, 256, 256)] = (jax.nn.silu(gt) * up).astype(BF)
+            gt = _dot(n, W[wrow(j, 0, D), ds(c, M, M)])
+            up = _dot(n, W[wrow(j, 0, D), ds(PC + c, M, M)])
+            act[rows, ds(j * PC + c, M, M)] = (jax.nn.silu(gt) * up).astype(BF)
             return 0
 
-        lax.fori_loop(0, (Z // 256) * (PC // 256), body, 0)
+        lax.fori_loop(0, (Z // M) * (PC // M), body, 0)
 
     dy, dyc, dloads = {}, {}, {}
 
     def down_y(p):
         c = pl.ds(p * S, S)
         dy[p] = [put(wd.at[:, c], dl.at[0, pl.ds(0, FP), c], YN),
-                 put(wo.at[:, c], dl.at[0, pl.ds(FP, HD // 2), c], YN)]
+                 put(wo.at[:, c], dl.at[0, pl.ds(FP, OC), c], YN)]
 
     def dslot(ky, p):
-        return ((ky * 3 + p) % 4) * 2 * S
+        return ((ky * 3 + p) % 4) * S2
 
     def down_load(ky, p):
         out = []
@@ -244,12 +249,12 @@
             if ky == 0 and kc == 0:
                 top, bot = wd, wo.at[:, c]
             else:
-                k = {(1, 0): 0, (0, 1): 1, (1, 1): 2}[ky, kc]
-                top, bot = dl.at[k], dl.at[k, pl.ds(FP, HD // 2), c]
+                k = ky + 2 * kc - 1
+                top, bot = dl.at[k], dl.at[k, pl.ds(FP, OC), c]
             to = pl.ds(dslot(ky, p) + kc * S, S)
-            out.append(load(top.at[ds(ix * (FP // 2), FP // 2, FP // 2), c], W.at[pl.ds(0, FP // 2), to]))
-            out.append(load(top.at[ds((1 - ix) * (FP // 2), FP // 2, FP // 2), c], W.at[pl.ds(FP // 2, FP // 2), to]))
-            out.append(load(bot, W.at[pl.ds(FP, HD // 2), to]))
+            out.append(load(top.at[ds(ix * FX, FX, FX), c], W.at[pl.ds(0, FX), to]))
+            out.append(load(top.at[ds((1 - ix) * FX, FX, FX), c], W.at[pl.ds(FX, FX), to]))
+            out.append(load(bot, W.at[pl.ds(FP, OC), to]))
         dloads[ky, p] = out
 
     def w_settle(j):
@@ -259,7 +264,7 @@
 
     def act_put(j, half):
         rows = zo if half else zr
-        acts[j, half] = put(act.at[rows, pl.ds(j * PC, PC)], act.at[rows, pl.ds(FP // 2 + j * PC, PC)], XN)
+        acts[j, half] = put(act.at[rows, pl.ds(j * PC, PC)], act.at[rows, pl.ds(FX + j * PC, PC)], XN)
 
     for j in range(PIECES):
         if j + 1 < PIECES:
@@ -288,35 +293,35 @@
         c.wait_recv()
     for p in range(3):
         down_load(0, p)
-    ol = load(o.at[ds(mine, R, R), :], N.at[:, pl.ds(0, HD // 2)])
+    ol = load(o.at[ds(mine, R, R), :], N.at[:, pl.ds(0, OC)])
 
     rs = {}
 
     def step(ky, p):
-        return (ky * 3 + p) * 2 * S
-
-    def down(ky, p, half, dst, at, i0=0, n=Z // 256):
+        return (ky * 3 + p) * S2
+
+    def down(ky, p, half, dst, at, i0=0, n=Z // M):
         def f(i, _):
-            c = pl.ds(dslot(ky, p), 2 * S)
-            rows = ds(half * Z + i * 256, 256, 256)
-            dst[ds(i * 256, 256, 256), pl.ds(at, 2 * S)] = (
-                _dot(act[rows, :], W[pl.ds(0, FP), c]) + _dot(N[rows, pl.ds(0, HD // 2)], W[pl.ds(FP, HD // 2), c]))
+            c = pl.ds(dslot(ky, p), S2)
+            rows = ds(half * Z + i * M, M, M)
+            dst[ds(i * M, M, M), pl.ds(at, S2)] = (
+                _dot(act[rows, :], W[pl.ds(0, FP), c]) + _dot(N[rows, pl.ds(0, OC)], W[pl.ds(FP, OC), c]))
             return 0
         lax.fori_loop(i0, i0 + n, f, 0)
 
     def parts(ky, p):
-        return ((0, 256), (256, 256)) if (ky, p) == (1, 2) else ((0, Z),)
+        return ((0, M), (M, M)) if (ky, p) == (1, 2) else ((0, Z),)
 
     def down_far(ky, p):
         for c in dloads[ky, p]:
             c.wait()
-        s = pl.ds(step(ky, p), 2 * S)
+        s = pl.ds(step(ky, p), S2)
         for r, n in parts(ky, p):
-            down(ky, p, 1 - z, ys, step(ky, p), r // 256, n // 256)
+            down(ky, p, 1 - z, ys, step(ky, p), r // M, n // M)
             rs[ky, p, r] = put(ys.at[pl.ds(r, n), s], yr.at[pl.ds(r, n), s], ZN)
 
     def near(ky, p):
-        return ((ky * 3 + p) % 2) * 2 * S
+        return ((ky * 3 + p) % 2) * S2
 
     def down_near(ky, p):
         down(ky, p, z, yo, near(ky, p))
@@ -326,33 +331,39 @@
 
     xx, xz, xf = {}, {}, {}
 
+    def finish_part(ky, p, r0, n):
+        rs[ky, p, r0].wait_recv()
+
+        def f(i, _):
+            r = ds(r0 + i * 64, 64, 64)
+            ra = ds(z * Z + r0 + i * 64, 64, 64)
+            for kc in range(2):
+                c = acol(ky, p, kc)
+                mine_y = yo[r, pl.ds(near(ky, p) + kc * S, S)]
+                A[ra, c] = (A[ra, c].astype(F32) + (mine_y + yr[r, pl.ds(step(ky, p) + kc * S, S)])).astype(BF)
+            return 0
+
+        lax.fori_loop(0, n // 64, f, 0)
+        rows = ds(z * Z + r0, n, n)
+        for kc in range(2):
+            xx[ky, p, kc, r0] = put(A.at[rows, acol(ky, p, kc)], A.at[rows, acol(ky, p, kc, 1)], XN)
+
     def finish(ky, p):
         for r0, n in parts(ky, p):
-            rs[ky, p, r0].wait_recv()
-
-            def f(i, _):
-                r = ds(r0 + i * 64, 64, 64)
-                ra = ds(z * Z + r0 + i * 64, 64, 64)
-                for kc in range(2):
-                    c = acol(ky, p, kc)
-                    mine_y = yo[r, pl.ds(near(ky, p) + kc * S, S)]
-                    A[ra, c] = (A[ra, c].astype(F32) + (mine_y + yr[r, pl.ds(step(ky, p) + kc * S, S)])).astype(BF)
-                return 0
-
-            lax.fori_loop(0, n // 64, f, 0)
-            rows = ds(z * Z + r0, n, n)
-            for kc in range(2):
-                xx[ky, p, kc, r0] = put(A.at[rows, acol(ky, p, kc)], A.at[rows, acol(ky, p, kc, 1)], XN)
+            finish_part(ky, p, r0, n)
 
     def z_own(ky, p):
         for kc in range(2):
             c = acol(ky, p, kc)
             xz[ky, p, kc] = put(A.at[zr, c], A.at[zr, c], ZN)
 
+    def x_got_part(ky, p, r0):
+        for kc in range(2):
+            xx[ky, p, kc, r0].wait_recv()
+
     def x_got(ky, p):
         for r0, _ in parts(ky, p):
-            for kc in range(2):
-                xx[ky, p, kc, r0].wait_recv()
+            x_got_part(ky, p, r0)
 
     def z_far(ky, p):
         for kc in range(2):
@@ -386,179 +397,193 @@
     finish(0, 1)
     down_near(1, 0)
     finish(0, 2)
+    z_own(0, 0)
+    z_own(0, 1)
 
     qyo, qyf, qcy, qloads = {}, {}, {}, {}
 
-    def tile(t, n=1):
-        return pl.ds(t * QT, n * QT)
+    def tile(t):
+        return pl.ds(t * QT, QT)
 
     def qw_y(gi):
-        t, n = QG[gi]
-        qyo[gi] = put(wq.at[:, ds(ix * QC + t * QT, n * QT, QT)], ql.at[2, :, tile(t, n)], YN)
-        qyf[gi] = put(ql.at[1, :, tile(t, n)], ql.at[3, :, tile(t, n)], YN)
+        qyo[gi] = put(wq.at[:, ds(ix * QC + gi * QT, QT, QT)], ql.at[2, :, tile(gi)], YN)
+        qyf[gi] = put(ql.at[1, :, tile(gi)], ql.at[3, :, tile(gi)], YN)
 
     def qw_ygot(gi):
-        t, n = QG[gi]
         qyo[gi].wait_recv()
-        a1 = put(ql.at[2, :, tile(t, n)], ql.at[6, :, tile(t, n)], CN)
+        a1 = put(ql.at[2, :, tile(gi)], ql.at[6, :, tile(gi)], CN)
         qyf[gi].wait_recv()
-        a2 = put(ql.at[3, :, tile(t, n)], ql.at[7, :, tile(t, n)], CN)
+        a2 = put(ql.at[3, :, tile(gi)], ql.at[7, :, tile(gi)], CN)
         qcy[gi] = (a1, a2)
 
     def slot(t, k):
         r, c = QSLOT[t]
         return W.at[pl.ds(r + k * B, B), pl.ds(c, QT)]
 
-    def qload(gi, ks):
-        t0, n = QG[gi]
-        for t in range(t0, t0 + n):
-            for k in ks:
-                src = wq.at[:, ds(ix * QC + t * QT, QT, QT)] if k == 0 else ql.at[k, :, tile(t)]
-                qloads.setdefault(t, []).append(load(src, slot(t, k)))
+    def qload(t, ks):
+        for k in ks:
+            src = ql.at[k, :, tile(t)] if k else wq.at[:, ds(ix * QC + t * QT, QT, QT)]
+            qloads.setdefault(t, []).append(load(src, slot(t, k)))
 
     qx.wait_recv()
     qc1 = put(ql.at[1], ql.at[5], CN)
-    for gi in range(len(QG)):
+    for gi in range(QN):
         qw_y(gi)
     qc0.wait_recv()
     qc1.wait_recv()
-    for gi in range(2):
-        qload(gi, (0, 1, 4, 5))
+    for gi in range(4):
+        qload(gi, EARLY)
 
     down_ygot(1)
     down_ready(1)
     down_far(1, 1)
-    for p in range(3):
-        z_own(0, p)
+    z_own(0, 2)
+    x_got(0, 0)
+    z_far(0, 0)
     finish(1, 0)
     down_near(1, 1)
-    qload(2, (0, 1, 4, 5))
-    for p in range(3):
-        x_got(0, p)
+    qload(4, EARLY)
+    x_got(0, 1)
+    x_got(0, 2)
     finish(1, 1)
     down_ygot(2)
     down_ready(2)
     down_far(1, 2)
-    for p in range(3):
-        z_far(0, p)
+    z_far(0, 1)
+    z_far(0, 2)
     for p in range(2):
         z_own(1, p)
     for p in range(2):
         x_got(1, p)
         z_far(1, p)
     down_near(1, 2)
+    def qw_ready(gi):
+        for c in qcy[gi]:
+            c.wait_recv()
+        qload(gi, LATE)
+
     qw_ygot(0)
-    finish(1, 2)
-    z_own(1, 2)
-    for c in qcy[0]:
-        c.wait_recv()
-    qload(0, (2, 3, 6, 7))
-    x_got(1, 2)
-    z_far(1, 2)
-    norm(z * Z, Z, 1)
+    qw_ready(0)
 
     qxr, qyr, qdr, qcr = {}, {}, {}, []
 
     def at(u, fy, fx):
-        half, t = (z if u < 5 else 1 - z), u % 5
+        far, r, n, t = UNITS[u]
+        half = 1 - z if far else z
         py = 1 - iy if fy else iy
         px = 1 - ix if fx else ix
-        return qo.at[ds(quarter(py, ic) + half * Z, Z, Z), ds(px * QC + t * QT, QT, QT)]
+        return qo.at[ds(quarter(py, ic) + half * Z + r, n, n), ds(px * QC + t * QT, QT, QT)]
 
     def unit(u):
-        t = u % 5
-        if u < 5:
-            for c in qloads[t]:
-                c.wait()
-        half = z if u < 5 else 1 - z
+        far, r0, n, t = UNITS[u]
+        for c in qloads.pop(t, ()):
+            c.wait()
+        base = (1 - z if far else z) * Z + r0
 
         def f(i, _):
             r, c = QSLOT[t]
             w = W[pl.ds(r, D), pl.ds(c, QT)]
-            to = qo.at[ds(mine + half * Z + i * 256, 256, 256), ds(ix * QC + t * QT, QT, QT)]
-            to[...] = _dot(N[ds(half * Z + i * 256, 256, 256), :], w).astype(BF)
+            to = qo.at[ds(mine + base + i * M, M, M), ds(ix * QC + t * QT, QT, QT)]
+            to[...] = _dot(N[ds(base + i * M, M, M), :], w).astype(BF)
             return 0
 
-        lax.fori_loop(0, Z // 256, f, 0)
+        lax.fori_loop(0, n // M, f, 0)
         ref = at(u, 0, 0)
         qxr[u] = put(ref, ref, XN)
         qyr[u] = put(ref, ref, YN)
         qcr.append(put(ref, ref, CN))
 
-    def got_x(u):
-        qxr[u].wait_recv()
-        ref = at(u, 0, 1)
-        if u in XFIRST:
-            qdr[u] = put(ref, ref, YN)
-        qcr.append(put(ref, ref, CN))
-
-    def got_y(u):
-        qyr[u].wait_recv()
-        ref = at(u, 1, 0)
-        if u not in XFIRST:
-            qdr[u] = put(ref, ref, XN)
-        qcr.append(put(ref, ref, CN))
-
-    def got_d(u):
-        qdr[u].wait_recv()
-        ref = at(u, 1, 1)
-        qcr.append(put(ref, ref, CN))
-
+    def got_x(*us):
+        for u in us:
+            qxr[u].wait_recv()
+            ref = at(u, 0, 1)
+            if u in XFIRST:
+                qdr[u] = put(ref, ref, YN)
+            qcr.append(put(ref, ref, CN))
+
+    def got_y(*us):
+        for u in us:
+            qyr[u].wait_recv()
+            ref = at(u, 1, 0)
+            if u not in XFIRST:
+                qdr[u] = put(ref, ref, XN)
+            qcr.append(put(ref, ref, CN))
+
+    def got_d(*us):
+        for u in us:
+            qdr[u].wait_recv()
+            ref = at(u, 1, 1)
+            qcr.append(put(ref, ref, CN))
+
+    finish(1, 2)
+    z_own(1, 2)
+    x_got_part(1, 2, 0)
+    qw_ygot(1)
+    norm(z * Z, M, 1)
     unit(0)
-    qw_ygot(1)
-    for c in qcy[1]:
-        c.wait_recv()
-    qload(1, (2, 3, 6, 7))
+    qw_ready(1)
+    x_got_part(1, 2, M)
+    z_far(1, 2)
+    norm(z * Z + M, M, 1)
     unit(1)
     unit(2)
-    got_x(0)
     qw_ygot(2)
-    for c in qcy[2]:
-        c.wait_recv()
-    qload(2, (2, 3, 6, 7))
+    qw_ready(2)
+    got_x(0, 1)
     unit(3)
+    qw_ygot(3)
+    qw_ready(3)
     unit(4)
+    got_x(2)
+    qw_ygot(4)
+    qw_ready(4)
+    unit(5)
     orow = ds(mine + z * Z, Z, Z)
     oy = put(A.at[zr, col(2)], xo.at[orow, :], YN)
     oyc = put(A.at[zr, col(6)], xo.at[orow, :], YCN)
-    got_y(0)
-    got_x(1)
-    got_y(1)
-    got_x(2)
-    got_y(2)
+    got_x(3)
+    got_y(0, 1)
+    got_x(4)
+    got_y(2, 3)
+    got_x(5)
+    got_y(4)
     for k in xz:
         xz[k].wait_recv()
+    got_y(5)
     for k in xf:
         xf[k].wait_recv()
     norm((1 - z) * Z, Z, 1)
-    unit(5)
     unit(6)
-    got_x(3)
-    got_y(3)
     unit(7)
     unit(8)
-    got_x(4)
-    got_y(4)
+    got_d(0, 1, 2)
     unit(9)
+    unit(10)
+    unit(11)
     oc = put(A.at[:, col(4)], xo.at[ds(mine, R, R), :], CN)
 
     def keep(i, _):
-        xo[ds(mine + i * 128, 128, 128), :] = A[ds(i * 128, 128, 128), col(0)]
+        xo[ds(mine + i * M, M, M), :] = A[ds(i * M, M, M), col(0)]
         return 0
 
-    lax.fori_loop(0, R // 128, keep, 0)
+    lax.fori_loop(0, R // M, keep, 0)
+    got_x(6)
     oy.wait_recv()
     r0 = ds(quarter(1 - iy, ic) + z * Z, Z, Z)
     ozy = put(xo.at[r0, :], xo.at[r0, :], ZN)
     oyc.wait_recv()
     r1 = ds(quarter(1 - iy, 1 - ic) + z * Z, Z, Z)
     ozc = put(xo.at[r1, :], xo.at[r1, :], ZN)
-    for u in range(5, 10):
-        got_x(u)
-        got_y(u)
-        got_d(u - 5)
-    for u in range(5, 10):
-        got_d(u)
+    got_d(3, 4, 5)
+    got_x(7)
+    got_y(6)
+    got_x(8)
+    got_y(7)
+    got_x(9)
+    got_y(8)
+    got_x(10, 11)
+    got_y(9, 10, 11)
+    got_d(*range(6, 12))
     for c in (oc, ozy, ozc):
         c.wait_recv()
     for c in qcr:
@@ -580,7 +605,7 @@
             out_specs=(vmem, vmem, hbm, hbm, hbm),
             scratch_shapes=[
                 pltpu.VMEM((R, D), BF), pltpu.VMEM((R, D), BF), pltpu.VMEM((2 * D, 2 * PC), BF),
-                pltpu.VMEM((R, FP), BF), pltpu.VMEM((Z, 12 * S), F32), pltpu.VMEM((Z, 12 * S), F32),
+                pltpu.VMEM((R, FP), BF), pltpu.VMEM((Z, 6 * S2), F32), pltpu.VMEM((Z, 6 * S2), F32),
                 pltpu.VMEM((Z, 4 * S), F32), pltpu.VMEM((8, D), F32),
                 pltpu.SemaphoreType.DMA((NREMOTE,)), pltpu.SemaphoreType.DMA((NREMOTE,)),
                 pltpu.SemaphoreType.DMA((NLOCAL,)),

time: 406 us -> 399 us (0.983)
  Pallas kernels: 394 us -> 387 us
    pallas_call x1, Pallas kernels: 394 us -> 387 us  [body(): pl.pallas_call(_kernel, out_shape=(pltpu.VMEM((T, B), BF), pltpu.VMEM((T,...]
where the time goes in v4:
time: 399 us
  Pallas kernels  387 us (97%)
  local copies, waits for them, and re-layouts  9.21 us (2%)
    pallas_call x1, Pallas kernels, body(): pl.pallas_call(_kernel, out_shape=(pltpu.VMEM((T, B), BF), pltpu.VMEM((T,...  387 us
    unnamed x2, local copies, waits for them, and re-layouts  9.21 us

profile of v4, /device:TPU:0, one launch (start us, length us, event | category | flops | bytes accessed | tf_op | source)
XLA Modules:
  0.0 398.6 jit_solution(12613296137707157017)
XLA Ops:
  0.6 1.4 broadcast_select_fusion.g
  2.0 387.3 %shard_map.104 = (bf16[4096,384]{1,0:T(8,128)(2,1)S(1)}, bf16[4096,2560]{1,0:T(8,128)(2,1)S(1)}, bf16[3,5632,384]{2,1,0:T(8,128)(2,1)}, bf16[8,384,1280]{2,1,0:T(8,128)(2,1)}, bf16[2,3072,1024]{2,1,0:T(8,128)(2,1)}) custom-call(bf16[4096,384]{1,0:T(8,128)(2,1)} %x.1, f32[8,384]{1,0:T(8,128)} %broadcast_select_fusion.g, bf16[384,4096]{1,0:T(8,128)(2,1)} %wg.1, ...), custom_call_target="tpu_custom_call" | custom-call | tf_op jit(solution)/shard_map/pallas_call | solution.py:600
  389.3 1.7 copy.13
  391.0 7.5 %copy.14 = bf16[4096,2560]{1,0:T(8,128)(2,1)} copy(bf16[4096,2560]{1,0:T(8,128)(2,1)S(1)} %get-tuple-element.7) | data formatting | bytes 41943040
  (1 shorter events, 0.0 us)

commit v5 on v4

--- a/solution.py
+++ b/solution.py
@@ -8,7 +8,7 @@
 EPS = 1e-6
 BF, F32 = jnp.bfloat16, jnp.float32
 MESH = pl.DeviceIdType.MESH
-NREMOTE, NLOCAL = 288, 128
+NREMOTE, NLOCAL, NWRITE = 288, 128, 8
 
 T, D, FF, HD, Q = 4096, 3072, 8192, 3072, 5120
 B = D // 8
@@ -36,7 +36,7 @@
     return jnp.dot(a, b, preferred_element_type=F32)
 
 
-def _kernel(x, g, wg, wu, wd, o, wo, wq, xo, qo, dl, ql, wh,
+def _kernel(x, ga, gb, wg, wu, wd, o, wo, wq, xo, qo, dl, ql, wh,
             A, N, W, act, ys, yr, yo, gv, send, recv, loc):
     h = lax.axis_index('h')
     z = lax.axis_index('f')
@@ -166,8 +166,9 @@
     w_load(0)
     w_load(1)
     w_x(0)
-    gs = [put(g, gv.at[:, col(k)], dev(k & 1, (k >> 1) & 1, k >> 2)) for k in range(1, 8)]
-    g0 = load(g, gv.at[:, col(0)])
+    gs = [put(v, gv.at[i, k], dev(k & 1, (k >> 1) & 1, k >> 2)) for k in range(1, 8) for i, v in enumerate((ga, gb))]
+    gv[0, 0] = ga[...]
+    gv[1, 0] = gb[...]
     w_yown(0)
     w_yown(1)
 
@@ -201,13 +202,12 @@
     zput(7)
     for c in gs:
         c.wait_recv()
-    g0.wait()
     x0.wait()
     for c in zs:
         c.wait_recv()
 
     def norm(row, n, gi):
-        gain = gv[gi:gi + 1, :]
+        gain = jnp.concatenate([gv[gi, k, i:i + 1, :] for k in range(8) for i in range(3)], 1)
 
         def body(i, _):
             rows = ds(row + i * 32, 32, 32)
@@ -591,29 +591,43 @@
     settle(list(sends))
 
 
+def _write(a, b, ao, bo, sem):
+    jobs = [(a, ao, pl.ds(0, T))] + [(b, bo, pl.ds(i * (T // NWRITE), T // NWRITE)) for i in range(NWRITE)]
+    copies = [pltpu.make_async_copy(s.at[r, :], d.at[r, :], sem.at[i]) for i, (s, d, r) in enumerate(jobs)]
+    for c in copies:
+        c.start()
+    for c in copies:
+        c.wait()
+
+
 def solution(mesh):
     def body(x, g1, g2, w_gate, w_up, w_down, o, w_o, w_qkv):
-        spread = lambda v: lax.broadcast_in_dim(v, (8, B), (1,))
-        g = jnp.where(lax.broadcasted_iota(jnp.int32, (8, B), 0) == 0, spread(g1), spread(g2))
         hbm, vmem = pl.BlockSpec(memory_space=pltpu.HBM), pl.BlockSpec(memory_space=pltpu.VMEM)
         keep = lambda v: pltpu.with_memory_space_constraint(v, pltpu.HBM)
         outs = pl.pallas_call(
             _kernel,
             out_shape=(pltpu.VMEM((T, B), BF), pltpu.VMEM((T, Q // 2), BF), pltpu.HBM((3, K2, B), BF),
                        pltpu.HBM((8, B, QC), BF), pltpu.HBM((2, D, 2 * PC), BF)),
-            in_specs=[hbm, vmem] + [hbm] * 6,
+            in_specs=[hbm, vmem, vmem] + [hbm] * 6,
             out_specs=(vmem, vmem, hbm, hbm, hbm),
             scratch_shapes=[
                 pltpu.VMEM((R, D), BF), pltpu.VMEM((R, D), BF), pltpu.VMEM((2 * D, 2 * PC), BF),
                 pltpu.VMEM((R, FP), BF), pltpu.VMEM((Z, 6 * S2), F32), pltpu.VMEM((Z, 6 * S2), F32),
-                pltpu.VMEM((Z, 4 * S), F32), pltpu.VMEM((8, D), F32),
+                pltpu.VMEM((Z, 4 * S), F32), pltpu.VMEM((2, 8, 3, 128), F32),
                 pltpu.SemaphoreType.DMA((NREMOTE,)), pltpu.SemaphoreType.DMA((NREMOTE,)),
                 pltpu.SemaphoreType.DMA((NLOCAL,)),
             ],
             compiler_params=pltpu.CompilerParams(collective_id=0, has_side_effects=True,
                                                  vmem_limit_bytes=VMEM_LIMIT),
-        )(keep(x), g, *[keep(v) for v in (w_gate, w_up, w_down, o, w_o, w_qkv)])
-        return outs[0], outs[1]
+        )(keep(x), g1.reshape(3, 128), g2.reshape(3, 128), *[keep(v) for v in (w_gate, w_up, w_down, o, w_o, w_qkv)])
+        return pl.pallas_call(
+            _write,
+            out_shape=tuple(jax.ShapeDtypeStruct(v.shape, v.dtype) for v in outs[:2]),
+            in_specs=[vmem, vmem],
+            out_specs=(hbm, hbm),
+            scratch_shapes=[pltpu.SemaphoreType.DMA((NWRITE + 1,))],
+            compiler_params=pltpu.CompilerParams(vmem_limit_bytes=4 * T * D // 12),
+        )(*[pltpu.with_memory_space_constraint(v, pltpu.VMEM) for v in outs[:2]])
 
     in_specs = (P(None, 'h'), P('h'), P('h'), P('h', 'f'), P('h', 'f'), P('f', 'h'),
                 P(None, 'f'), P('f', 'h'), P('h', 'f'))

time: 399 us -> 396 us (level)
  local copies, waits for them, and re-layouts: 9.21 us -> 0 us
  Pallas kernels: 387 us -> 395 us
    unnamed x2 -> x0, local copies, waits for them, and re-layouts: 9.21 us -> none
    pallas_call x0 -> x1, Pallas kernels: none -> 8.2 us  [body(): pl.pallas_call(_write, out_shape=tuple((jax.ShapeDtypeStruct(v.shape, v.d...]
where the time goes in v5:
time: 396 us
  Pallas kernels  395 us (100%)
    pallas_call x1, Pallas kernels, body(): pl.pallas_call(_kernel, out_shape=(pltpu.VMEM((T, B), BF), pltpu.VMEM((T,...  387 us
    pallas_call x1, Pallas kernels, body(): pl.pallas_call(_write, out_shape=tuple((jax.ShapeDtypeStruct(v.shape, v.d...  8.2 us

profile of v5, /device:TPU:0, one launch (start us, length us, event | category | flops | bytes accessed | tf_op | source)
XLA Modules:
  0.0 395.5 jit_solution(6632393519940755842)
XLA Ops:
  0.6 386.5 %shard_map.104 = (bf16[4096,384]{1,0:T(8,128)(2,1)S(1)}, bf16[4096,2560]{1,0:T(8,128)(2,1)S(1)}, bf16[3,5632,384]{2,1,0:T(8,128)(2,1)}, bf16[8,384,1280]{2,1,0:T(8,128)(2,1)}, bf16[2,3072,1024]{2,1,0:T(8,128)(2,1)}) custom-call(bf16[4096,384]{1,0:T(8,128)(2,1)} %x.1, f32[3,128]{1,0:T(4,128)} %bitcast.2, f32[3,128]{1,0:T(4,128)} %bitcast.3, ...), custom_call_target="tpu_custom_call" | custom-call | tf_op jit(solution)/shard_map/pallas_call | solution.py:607
  387.1 8.2 %shard_map.105 = (bf16[4096,384]{1,0:T(8,128)(2,1)}, bf16[4096,2560]{1,0:T(8,128)(2,1)}) custom-call(bf16[4096,384]{1,0:T(8,128)(2,1)S(1)} %get-tuple-element.4.a, bf16[4096,2560]{1,0:T(8,128)(2,1)S(1)} %get-tuple-element.5.b), custom_call_target="tpu_custom_call" | custom-call | tf_op jit(solution)/shard_map/pallas_call | solution.py:623

commit v6 on v5

--- a/solution.py
+++ b/solution.py
@@ -8,7 +8,7 @@
 EPS = 1e-6
 BF, F32 = jnp.bfloat16, jnp.float32
 MESH = pl.DeviceIdType.MESH
-NREMOTE, NLOCAL, NWRITE = 288, 128, 8
+NREMOTE, NSEND, NLOCAL, NWRITE = 239, 96, 48, 8
 
 T, D, FF, HD, Q = 4096, 3072, 8192, 3072, 5120
 B = D // 8
@@ -50,20 +50,23 @@
 
     XN, YN, CN, YCN, ZN = dev(1, 0, 0), dev(0, 1, 0), dev(0, 0, 1), dev(0, 1, 1), {'f': 1 - z}
     count = [0, 0]
-    sends = []
+    sends, every = [], []
 
     def put(src, dst, to):
         i = count[0]
         count[0] += 1
-        c = pltpu.make_async_remote_copy(src, dst, send.at[i], recv.at[i], device_id=to, device_id_type=MESH)
+        if i >= NSEND:
+            settle([c for c in sends if c is every[i - NSEND]])
+        c = pltpu.make_async_remote_copy(src, dst, send.at[i % NSEND], recv.at[i], device_id=to, device_id_type=MESH)
         c.start()
+        every.append(c)
         sends.append(c)
         return c
 
     def load(src, dst):
         i = count[1]
         count[1] += 1
-        c = pltpu.make_async_copy(src, dst, loc.at[i])
+        c = pltpu.make_async_copy(src, dst, loc.at[i % NLOCAL])
         c.start()
         return c
 
@@ -614,7 +617,7 @@
                 pltpu.VMEM((R, D), BF), pltpu.VMEM((R, D), BF), pltpu.VMEM((2 * D, 2 * PC), BF),
                 pltpu.VMEM((R, FP), BF), pltpu.VMEM((Z, 6 * S2), F32), pltpu.VMEM((Z, 6 * S2), F32),
                 pltpu.VMEM((Z, 4 * S), F32), pltpu.VMEM((2, 8, 3, 128), F32),
-                pltpu.SemaphoreType.DMA((NREMOTE,)), pltpu.SemaphoreType.DMA((NREMOTE,)),
+                pltpu.SemaphoreType.DMA((NSEND,)), pltpu.SemaphoreType.DMA((NREMOTE,)),
                 pltpu.SemaphoreType.DMA((NLOCAL,)),
             ],
             compiler_params=pltpu.CompilerParams(collective_id=0, has_side_effects=True,

time: 396 us -> 393 us (level)
  no operation moved by 1% of the time
where the time goes in v6:
time: 393 us
  Pallas kernels  392 us (100%)
    pallas_call x1, Pallas kernels, body(): pl.pallas_call(_kernel, out_shape=(pltpu.VMEM((T, B), BF), pltpu.VMEM((T,...  384 us
    pallas_call x1, Pallas kernels, body(): pl.pallas_call(_write, out_shape=tuple((jax.ShapeDtypeStruct(v.shape, v.d...  8.2 us

profile of v6, /device:TPU:0, one launch (start us, length us, event | category | flops | bytes accessed | tf_op | source)
XLA Modules:
  0.0 392.6 jit_solution(3191567538052217612)
XLA Ops:
  0.6 383.6 %shard_map.104 = (bf16[4096,384]{1,0:T(8,128)(2,1)S(1)}, bf16[4096,2560]{1,0:T(8,128)(2,1)S(1)}, bf16[3,5632,384]{2,1,0:T(8,128)(2,1)}, bf16[8,384,1280]{2,1,0:T(8,128)(2,1)}, bf16[2,3072,1024]{2,1,0:T(8,128)(2,1)}) custom-call(bf16[4096,384]{1,0:T(8,128)(2,1)} %x.1, f32[3,128]{1,0:T(4,128)} %bitcast.2, f32[3,128]{1,0:T(4,128)} %bitcast.3, ...), custom_call_target="tpu_custom_call" | custom-call | tf_op jit(solution)/shard_map/pallas_call | solution.py:610
  384.3 8.2 %shard_map.105 = (bf16[4096,384]{1,0:T(8,128)(2,1)}, bf16[4096,2560]{1,0:T(8,128)(2,1)}) custom-call(bf16[4096,384]{1,0:T(8,128)(2,1)S(1)} %get-tuple-element.4.a, bf16[4096,2560]{1,0:T(8,128)(2,1)S(1)} %get-tuple-element.5.b), custom_call_target="tpu_custom_call" | custom-call | tf_op jit(solution)/shard_map/pallas_call | solution.py:626

commit v7 on v6

--- a/solution.py
+++ b/solution.py
@@ -8,7 +8,7 @@
 EPS = 1e-6
 BF, F32 = jnp.bfloat16, jnp.float32
 MESH = pl.DeviceIdType.MESH
-NREMOTE, NSEND, NLOCAL, NWRITE = 239, 96, 48, 8
+NREMOTE, NSEND, NLOCAL, NWRITE = 239, 64, 48, 8
 
 T, D, FF, HD, Q = 4096, 3072, 8192, 3072, 5120
 B = D // 8

time: 393 us -> 393 us (level)
  no operation moved by 1% of the time
where the time goes in v7:
time: 393 us; the launch traced here: 392 us
  Pallas kernels  392 us (100%)
    pallas_call x1, Pallas kernels, body(): pl.pallas_call(_kernel, out_shape=(pltpu.VMEM((T, B), BF), pltpu.VMEM((T,...  383 us
    pallas_call x1, Pallas kernels, body(): pl.pallas_call(_write, out_shape=tuple((jax.ShapeDtypeStruct(v.shape, v.d...  8.2 us

profile of v7, /device:TPU:0, one launch (start us, length us, event | category | flops | bytes accessed | tf_op | source)
XLA Modules:
  0.0 392.4 jit_solution(15395641595128497344)
XLA Ops:
  0.6 383.4 %shard_map.104 = (bf16[4096,384]{1,0:T(8,128)(2,1)S(1)}, bf16[4096,2560]{1,0:T(8,128)(2,1)S(1)}, bf16[3,5632,384]{2,1,0:T(8,128)(2,1)}, bf16[8,384,1280]{2,1,0:T(8,128)(2,1)}, bf16[2,3072,1024]{2,1,0:T(8,128)(2,1)}) custom-call(bf16[4096,384]{1,0:T(8,128)(2,1)} %x.1, f32[3,128]{1,0:T(4,128)} %bitcast.2, f32[3,128]{1,0:T(4,128)} %bitcast.3, ...), custom_call_target="tpu_custom_call" | custom-call | tf_op jit(solution)/shard_map/pallas_call | solution.py:610
  384.0 8.2 %shard_map.105 = (bf16[4096,384]{1,0:T(8,128)(2,1)}, bf16[4096,2560]{1,0:T(8,128)(2,1)}) custom-call(bf16[4096,384]{1,0:T(8,128)(2,1)S(1)} %get-tuple-element.4.a, bf16[4096,2560]{1,0:T(8,128)(2,1)S(1)} %get-tuple-element.5.b), custom_call_target="tpu_custom_call" | custom-call | tf_op jit(solution)/shard_map/pallas_call | solution.py:626
